TPU v7x, 16 devices: a whole 2x2x2 slice. The times are simulated.
16 devices in a mesh: dp: 4 (over z, y), tp: 4 (over x, core).
Axes of the slice: x: 2, y: 2, z: 2, core: 2. Of those that a mesh axis runs over, the one named last changes fastest.
Arguments:
- hidden: bfloat16 [4, 128, 4096], P('dp'), parts along dimension 0
- ln_gain: float32 [4096], replicated
- ln_bias: float32 [4096], replicated
- embedding: bfloat16 [50688, 4096], P('tp')
- targets: int32 [4, 128], P('dp'), parts along dimension 0
- score_mask: int32 [4, 128], P('dp'), parts along dimension 0
Outputs:
- output 1: float32 [4, 128], P('dp'), parts along dimension 0
- output 2: float32 [4, 128], P('dp'), parts along dimension 0
- output 3: float32 [4], P('dp'), parts along dimension 0
- output 4: float32 [4, 128], P('dp'), parts along dimension 0
There are 4 independent parts. A program takes and returns all parts, laid end to end along the dimension named above; an argument that names none is the same for every part.
All inputs are finite; a program needn't handle non-finite values.
Results may differ from a plain program's by a relative error of at most 0.001.
Values sent between devices are 32-bit elements.
A program may use at most 1 GiB of HBM per device.

v0:
```python
import jax
import jax.numpy as jnp
from jax import lax
from jax.sharding import PartitionSpec as P

OPT_VOCAB = 50272
LN_EPS = 1e-5


def layer_norm(hidden, ln_gain, ln_bias):
    hidden_f = hidden.astype(jnp.float32)
    row_mean = jnp.mean(hidden_f, axis=-1, keepdims=True)
    centered = hidden_f - row_mean
    row_var = jnp.mean(centered * centered, axis=-1, keepdims=True)
    return (centered * lax.rsqrt(row_var + LN_EPS) * ln_gain + ln_bias).astype(jnp.bfloat16)


def solution(mesh):
    def local_part(hidden, ln_gain, ln_bias, embedding, targets, score_mask):
        shard_rows = embedding.shape[0]
        vocab_ids = lax.axis_index("tp") * shard_rows + jnp.arange(shard_rows)
        normed = layer_norm(hidden, ln_gain, ln_bias)
        logits = jnp.einsum("bsd,vd->bsv", normed, embedding, preferred_element_type=jnp.float32)
        logits = jnp.where(vocab_ids < OPT_VOCAB, logits, -jnp.inf)
        row_max = lax.pmax(jnp.max(logits, axis=-1), "tp")
        exp_sum = jnp.sum(jnp.exp(logits - row_max[..., None]), axis=-1)
        target_part = jnp.sum(jnp.where(vocab_ids == targets[..., None], logits, 0.0), axis=-1)
        combined = lax.psum(jnp.stack([exp_sum, target_part]), "tp")
        log_norm = row_max + jnp.log(combined[0])
        token_logp = (combined[1] - log_norm) * score_mask.astype(jnp.float32)
        return log_norm, token_logp, jnp.sum(token_logp, axis=-1), row_max - log_norm

    row_spec = P("dp", None)
    return jax.shard_map(local_part, mesh=mesh, in_specs=(P("dp", None, None), P(), P(), P("tp", None), row_spec, row_spec), out_specs=(row_spec, row_spec, P("dp"), row_spec), check_vma=False)
```

profile of v0, /device:TPU:0, one launch (start us, length us, event | category | flops | bytes accessed | tf_op | source)
XLA Modules:
  0.0 69.2 jit_solution(160989468342699617)
XLA Ops:
  0.7 1.5 %convert_reduce_fusion = f32[128]{0:T(128)S(1)} fusion(bf16[1,128,4096]{2,1,0:T(8,128)(2,1)} %param.6), kind=kLoop, calls=%fused_computation.4 | loop fusion | flops 1048448 | bytes 1049088 | tf_op jit(solution)/shard_map/reduce_sum | solution.py:12
  2.1 1.7 %fusion.2 = f32[128]{0:T(128)S(1)} fusion(bf16[1,128,4096]{2,1,0:T(8,128)(2,1)} %param.6, f32[128]{0:T(128)S(1)} %broadcast_multiply_fusion), kind=kLoop, calls=%fused_computation.7 | loop fusion | flops 2097024 | bytes 1049600 | tf_op jit(solution)/shard_map/reduce_sum | solution.py:14
  3.8 0.0 copy-start.2
  3.8 44.8 %fusion.20 = (f32[128]{0:T(128)S(1)}, f32[128,12672]{1,0:T(8,128)}) fusion(bf16[12672,4096]{1,0:T(8,128)(2,1)} %param.9, bf16[1,128,4096]{2,1,0:T(8,128)(2,1)} %param.6, f32[4096]{0:T(1024)} %param.8, f32[4096]{0:T(1024)} %param.7, f32[128]{0:T(128)S(1)} %add_rsqrt_fusion, f32[128]{0:T(128)S(1)} %broadcast_multiply_fusion, ...), kind=kOutput, calls=%fused_computation.29 | convolution fusion | flops 13293944832 | bytes 111392640 | tf_op jit(solution)/shard_map/bsd,vd->bsv/dot_general | solution.py:23
  48.6 0.0 copy-start.1
  48.6 8.6 %pmax.7 = f32[1,128]{1,0:T(1,128)S(1)} all-reduce(f32[1,128]{1,0:T(1,128)S(1)} %bitcast.31), channel_id=1, replica_groups=mesh['dp'=4,'tp'=4] {'tp'}, use_global_device_ids=true, to_apply=%region_3.4 | all-reduce | flops 128 | bytes 1024 | tf_op jit(solution)/shard_map/pmax | solution.py:25
  57.2 0.0 copy-done.2
  57.2 4.6 %exponential_reduce_fusion = (f32[128]{0:T(128)S(1)}, f32[128]{0:T(128)S(1)}) fusion(f32[128,12672]{1,0:T(8,128)} %get-tuple-element.11, f32[128]{0:T(128)S(1)} %bitcast.27, s32[128]{0:T(128)S(1)} %bitcast.30, s32[12672]{0:T(1024)S(1)} %iota_add_fusion), kind=kLoop, calls=%fused_computation.2 | loop fusion | flops 8109824 | bytes 6540800 | tf_op jit(solution)/shard_map/reduce_sum | solution.py:26
  61.8 5.8 %psum.7 = f32[2,1,128]{2,1,0:T(1,128)S(1)} all-reduce(f32[2,1,128]{2,1,0:T(1,128)S(1)} %pad_maximum_fusion), channel_id=1, replica_groups=mesh['dp'=4,'tp'=4] {'tp'}, use_global_device_ids=true, to_apply=%region_6.7 | all-reduce | flops 256 | bytes 2048 | tf_op jit(solution)/shard_map/psum | solution.py:28
  67.6 0.5 fusion.16
  68.1 0.0 copy-start
  68.1 0.0 copy-done.1
  68.1 1.1 %fusion.18 = (f32[]{:T(128)}, f32[1,128]{1,0:T(1,128)}) fusion(s32[1,128]{1,0:T(1,128)S(1)} %copy-done.1, f32[1,128]{1,0:T(1,128)S(1)} %get-tuple-element.7, f32[2,1,128]{2,1,0:T(1,128)S(1)} %psum.7), kind=kLoop, calls=%fused_computation.28 | loop fusion | flops 511 | bytes 2052 | tf_op jit(solution)/shard_map/reduce_sum | solution.py:31
  69.2 0.0 copy-done
  (5 shorter events, 0.0 us)
Async XLA Ops:
  3.8 53.4 %copy-start.2 = (s32[1,128]{1,0:T(1,128)S(1)}, s32[1,128]{1,0:T(1,128)}, u32[]{:S(2)}) copy-start(s32[1,128]{1,0:T(1,128)} %param.10) | copy-start | bytes 1540
  48.6 19.6 %copy-start.1 = (s32[1,128]{1,0:T(1,128)S(1)}, s32[1,128]{1,0:T(1,128)}, u32[]{:S(2)}) copy-start(s32[1,128]{1,0:T(1,128)} %param.11) | copy-start | bytes 1540
  68.1 1.1 %copy-start = (f32[1,128]{1,0:T(1,128)}, f32[1,128]{1,0:T(1,128)S(1)}, u32[]{:S(2)}) copy-start(f32[1,128]{1,0:T(1,128)S(1)} %get-tuple-element.7) | copy-start | bytes 1540
where the time goes:
time: 69.7 us; the launch traced here: 69.2 us
  matrix products  44.8 us (64%)
  blocking collectives  14.4 us (21%)
  other arithmetic  9.41 us (14%)
    dot_general x1, matrix products, local_part(): jnp.einsum('bsd,vd->bsv', normed, embedding, preferred_element_type=jnp.f...  44.8 us
    pmax x1, blocking collectives, local_part(): row_max = lax.pmax(jnp.max(logits, axis=-1), 'tp')  8.61 us
    psum x1, blocking collectives, local_part(): combined = lax.psum(jnp.stack([exp_sum, target_part]), 'tp')  5.76 us
    reduce_sum x1, other arithmetic, local_part(): exp_sum = jnp.sum(jnp.exp(logits - row_max[..., None]), axis=-1)  4.62 us
    reduce_sum x1, other arithmetic, layer_norm(): row_var = jnp.mean(centered * centered, axis=-1, keepdims=True)  1.65 us
    reduce_sum x1, other arithmetic, layer_norm(): row_mean = jnp.mean(hidden_f, axis=-1, keepdims=True)  1.45 us

commit v1 on v0

v1 whole, which is shorter than its diff:
```python
import functools

import jax
import jax.numpy as jnp
from jax import lax
from jax.experimental import pallas as pl
from jax.experimental.pallas import tpu as pltpu
from jax.sharding import PartitionSpec as P

OPT_VOCAB = 50272
LN_EPS = 1e-5
BLOCK = 384
SLOTS = 6
MESH = pl.DeviceIdType.MESH
NEG_INF = float("-inf")


def kernel(n_tp, x_hbm, gain_ref, bias_ref, emb_hbm, tgt_ref, msk_ref,
           norm_ref, logp_ref, top_ref, seq_ref,
           x_buf, h_buf, e_buf, m_acc, s_acc, t_acc, send_buf, recv_buf,
           x_sem, e_sem, send_sem, recv_sem):
    dp, tp = lax.axis_index("dp"), lax.axis_index("tp")
    rows = emb_hbm.shape[0]
    tokens = x_buf.shape[0]
    n_blocks = rows // BLOCK
    first_row = tp * rows

    def fetch(i, slot):
        return pltpu.make_async_copy(emb_hbm.at[pl.ds(i * BLOCK, BLOCK)], e_buf.at[slot], e_sem.at[slot])

    x_copy = pltpu.make_async_copy(x_hbm.at[0], x_buf, x_sem)
    x_copy.start()
    for s in range(SLOTS):
        fetch(s, s).start()

    barrier = pltpu.get_barrier_semaphore()
    for k in range(1, n_tp):
        pl.semaphore_signal(barrier, inc=1, device_id={"dp": dp, "tp": lax.rem(tp + k, n_tp)}, device_id_type=MESH)

    x_copy.wait()
    gain, bias = gain_ref[...], bias_ref[...]

    def norm_rows(r, carry):
        sl = pl.ds(pl.multiple_of(r * 16, 16), 16)
        x = x_buf[sl, :].astype(jnp.float32)
        mean = jnp.mean(x, axis=-1, keepdims=True)
        c = x - mean
        var = jnp.mean(c * c, axis=-1, keepdims=True)
        h_buf[sl, :] = (c * lax.rsqrt(var + LN_EPS) * gain + bias).astype(jnp.bfloat16)
        return carry

    lax.fori_loop(0, tokens // 16, norm_rows, 0)

    m_acc[...] = jnp.full_like(m_acc, NEG_INF)
    s_acc[...] = jnp.zeros_like(s_acc)
    t_acc[...] = jnp.zeros_like(t_acc)
    target = tgt_ref[...] - first_row

    def consume(i, masked):
        slot = lax.rem(i, SLOTS)
        fetch(i, slot).wait()
        z = lax.dot_general(e_buf[slot], h_buf[...], (((1,), (1,)), ((), ())), preferred_element_type=jnp.float32)
        z = z.reshape(BLOCK // 8, 8, tokens)
        row = (lax.broadcasted_iota(jnp.int32, z.shape, 0) * 8 + lax.broadcasted_iota(jnp.int32, z.shape, 1)) + i * BLOCK
        if masked:
            z = jnp.where(row < OPT_VOCAB - first_row, z, NEG_INF)
        t_acc[...] += jnp.sum(jnp.where(row == target[None], z, 0.0), axis=0)
        m_old = m_acc[...]
        m_new = jnp.maximum(m_old, jnp.max(z, axis=0))
        safe = jnp.where(m_new == NEG_INF, 0.0, m_new) if masked else m_new
        s_acc[...] = s_acc[...] * jnp.exp(m_old - safe) + jnp.sum(jnp.exp(z - safe[None]), axis=0)
        m_acc[...] = m_new

    n_plain = (rows - 768) // BLOCK

    def step(i, carry):
        consume(i, False)

        @pl.when(i + SLOTS < n_blocks)
        def _():
            fetch(i + SLOTS, lax.rem(i, SLOTS)).start()
        return carry

    lax.fori_loop(0, n_plain, step, 0)

    def last(i, carry):
        consume(i, True)
        return carry
    lax.fori_loop(n_plain, n_blocks, last, 0)

    m8 = m_acc[...]
    m1 = jnp.max(m8, axis=0, keepdims=True)
    s1 = jnp.sum(s_acc[...] * jnp.exp(m8 - m1), axis=0, keepdims=True)
    t1 = jnp.sum(t_acc[...], axis=0, keepdims=True)
    send_buf[0:1, :] = m1
    send_buf[1:2, :] = s1
    send_buf[2:3, :] = t1
    pl.semaphore_wait(barrier, n_tp - 1)
    copies = []
    for k in range(1, n_tp):
        copies.append(pltpu.make_async_remote_copy(
            src_ref=send_buf, dst_ref=recv_buf.at[k - 1], send_sem=send_sem.at[k - 1], recv_sem=recv_sem.at[k - 1],
            device_id={"dp": dp, "tp": lax.rem(tp + k, n_tp)}, device_id_type=MESH))
    for c in copies:
        c.start()
    for c in copies:
        c.wait_recv()
    ms, ss, ts = [m1], [s1], [t1]
    for k in range(1, n_tp):
        ms.append(recv_buf[k - 1, 0:1, :])
        ss.append(recv_buf[k - 1, 1:2, :])
        ts.append(recv_buf[k - 1, 2:3, :])
    m = functools.reduce(jnp.maximum, ms)
    total = sum(s * jnp.exp(mm - m) for s, mm in zip(ss, ms))
    z_t = sum(ts)
    norm = m + jnp.log(total)
    logp = (z_t - norm) * msk_ref[...].astype(jnp.float32)
    norm_ref[...] = norm
    logp_ref[...] = logp
    top_ref[...] = m - norm
    seq_ref[...] = jnp.broadcast_to(jnp.sum(logp, axis=-1, keepdims=True), logp.shape)
    for c in copies:
        c.wait_send()


def solution(mesh):
    n_tp = mesh.shape["tp"]

    def local_part(hidden, ln_gain, ln_bias, embedding, targets, score_mask):
        _, tokens, width = hidden.shape
        row = jax.ShapeDtypeStruct((1, tokens), jnp.float32)
        vmem = pl.BlockSpec(memory_space=pltpu.VMEM)
        hbm = pl.BlockSpec(memory_space=pl.ANY)
        norm, logp, top, seq = pl.pallas_call(
            functools.partial(kernel, n_tp),
            out_shape=(row, row, row, row),
            in_specs=[hbm, vmem, vmem, hbm, vmem, vmem],
            out_specs=(vmem, vmem, vmem, vmem),
            scratch_shapes=[
                pltpu.VMEM((tokens, width), jnp.bfloat16),
                pltpu.VMEM((tokens, width), jnp.bfloat16),
                pltpu.VMEM((SLOTS, BLOCK, width), jnp.bfloat16),
                pltpu.VMEM((8, tokens), jnp.float32),
                pltpu.VMEM((8, tokens), jnp.float32),
                pltpu.VMEM((8, tokens), jnp.float32),
                pltpu.VMEM((8, tokens), jnp.float32),
                pltpu.VMEM((n_tp - 1, 8, tokens), jnp.float32),
                pltpu.SemaphoreType.DMA,
                pltpu.SemaphoreType.DMA((SLOTS,)),
                pltpu.SemaphoreType.DMA((n_tp - 1,)),
                pltpu.SemaphoreType.DMA((n_tp - 1,)),
            ],
            compiler_params=pltpu.CompilerParams(collective_id=0, has_side_effects=True, vmem_limit_bytes=60 << 20),
        )(hidden, ln_gain.reshape(1, width), ln_bias.reshape(1, width), embedding, targets, score_mask)
        return norm, logp, seq[0, :1], top

    row_spec = P("dp", None)
    return jax.shard_map(local_part, mesh=mesh, in_specs=(P("dp", None, None), P(), P(), P("tp", None), row_spec, row_spec), out_specs=(row_spec, row_spec, P("dp"), row_spec), check_vma=False)
```

time: 69.7 us -> 54.7 us (0.78)
  Pallas kernels: 0 us -> 48.7 us
  matrix products: 44.8 us -> 0 us
  blocking collectives: 14.4 us -> 0 us
  other arithmetic: 9.41 us -> 0 us
  local copies, waits for them, and re-layouts: 0.01 us -> 3.42 us
  between operations: 0.67 us -> 2.38 us
    pallas_call x0 -> x1, Pallas kernels: none -> 48.7 us  [local_part(): pl.pallas_call(functools.partial(kernel, n_tp), out_shape=(row, row, row,...]
    dot_general x1 -> x0, matrix products: 44.8 us -> none  [local_part(): jnp.einsum('bsd,vd->bsv', normed, embedding, preferred_element_type=jnp.f...]
    reduce_sum x4 -> x0, other arithmetic: 8.84 us -> none  [the longest x1 4.62 us: local_part(): exp_sum = jnp.sum(jnp.exp(logits - row_max[..., None]), axis=-1)]
    pmax x1 -> x0, blocking collectives: 8.61 us -> none  [local_part(): row_max = lax.pmax(jnp.max(logits, axis=-1), 'tp')]
    psum x1 -> x0, blocking collectives: 5.76 us -> none  [local_part(): combined = lax.psum(jnp.stack([exp_sum, target_part]), 'tp')]
    unnamed x6 -> x3, local copies, waits for them, and re-layouts: 0.01 us -> 3.42 us
where the time goes in v1:
time: 54.7 us; the launch traced here: 54.5 us
  Pallas kernels  48.7 us (89%)
  local copies, waits for them, and re-layouts  3.42 us (6%)
  between operations  2.38 us (4%)
    pallas_call x1, Pallas kernels, local_part(): pl.pallas_call(functools.partial(kernel, n_tp), out_shape=(row, row, row,...  48.7 us
    unnamed x3, local copies, waits for them, and re-layouts  3.42 us

profile of v1, /device:TPU:0, one launch (start us, length us, event | category | flops | bytes accessed | tf_op | source)
XLA Modules:
  0.0 54.5 jit_solution(7800642759408411454)
XLA Ops:
  0.6 48.7 %shard_map.93 = (f32[1,128]{1,0:T(1,128)}, f32[1,128]{1,0:T(1,128)}, f32[1,128]{1,0:T(1,128)}, f32[1,128]{1,0:T(1,128)}) custom-call(bf16[1,128,4096]{2,1,0:T(8,128)(2,1)} %x_hbm.1, f32[1,4096]{1,0:T(1,128)} %bitcast.4, f32[1,4096]{1,0:T(1,128)} %bitcast.5, bf16[12672,4096]{1,0:T(8,128)(2,1)} %emb_hbm.1, s32[1,128]{1,0:T(1,128)} %tgt_ref.1, s32[1,128]{1,0:T(1,128)} %msk_ref.1), custom_call_target="tpu_custom_call" | custom-call | tf_op jit(solution)/shard_map/pallas_call | solution.py:134
  49.3 1.1 %copy.14 = f32[1,128]{1,0:T(1,128)} copy(f32[1,128]{1,0:T(1,128)} %get-tuple-element.16) | data formatting | bytes 1024
  50.4 1.1 %copy.15 = f32[1,128]{1,0:T(1,128)} copy(f32[1,128]{1,0:T(1,128)} %get-tuple-element.17) | data formatting | bytes 1024
  52.2 1.2 %copy.17 = f32[1,128]{1,0:T(1,128)} copy(f32[1,128]{1,0:T(1,128)} %get-tuple-element.19) | data formatting | bytes 1024

commit v2 on v0

v2 whole, which is shorter than its diff:
```python
import functools

import jax
import jax.numpy as jnp
from jax import lax
from jax.experimental import pallas as pl
from jax.experimental.pallas import tpu as pltpu
from jax.sharding import PartitionSpec as P

OPT_VOCAB = 50272
LN_EPS = 1e-5
CHUNK = 512
SHARED = 5632
MESH = pl.DeviceIdType.MESH
NEG_INF = float("-inf")
NT = (((1,), (1,)), ((), ()))


def kernel(n_tp, x_hbm, gain_ref, bias_ref, emb_hbm, tgt_ref, msk_ref, out_ref,
           x_buf, h_buf, hs_buf, fr_buf, e_buf, z_buf, zs_buf, tg_send, tg_recv, own_send, far_send, own_recv, y_recv, z_recv,
           x_sem, s_sem, e_sem, hs_sem, hr_sem, rs_sem, rr_sem, ts_sem, tr_sem, ss_sem, sr_sem):
    dp, tp = lax.axis_index("dp"), lax.axis_index("tp")
    rows, width = emb_hbm.shape
    tokens = x_buf.shape[0]
    half = tokens // 2
    n_chunks = width // CHUNK
    single = rows - 2 * SHARED
    per_slot = SHARED // single
    first_single = n_chunks - pl.cdiv(n_chunks, per_slot)
    core, y, z = tp % 2, dp % 2, dp // 2
    parity = (y + z) % 2
    dp_y, dp_z = dp + 1 - 2 * y, dp + 2 - 4 * z
    dp_far = dp_y + core * (dp_z - dp_y)
    tp_other = tp + 1 - 2 * core
    first_row = tp * rows
    shared_row = pl.multiple_of(parity * SHARED, 16)
    mine = pl.ds(pl.multiple_of(core * half, half), half)

    def fetch_x():
        return pltpu.make_async_copy(x_hbm.at[0], x_buf, x_sem)

    def fetch_single(c):
        src = emb_hbm.at[pl.ds(2 * SHARED, single), pl.ds(pl.multiple_of(c * CHUNK, CHUNK), CHUNK)]
        return pltpu.make_async_copy(src, single_ref(c), s_sem.at[c])

    def single_ref(c):
        return e_buf.at[first_single + c // per_slot, pl.ds(pl.multiple_of(c % per_slot * single, 16), single)]

    def fetch_shared(c):
        src = emb_hbm.at[pl.ds(shared_row, SHARED), pl.ds(pl.multiple_of(c * CHUNK, CHUNK), CHUNK)]
        return pltpu.make_async_copy(src, e_buf.at[c], e_sem.at[c])

    def send_h(c):
        return pltpu.make_async_remote_copy(hs_buf.at[c], fr_buf.at[c, mine], hs_sem.at[c], hr_sem.at[c], device_id={"dp": dp_far, "tp": tp}, device_id_type=MESH)

    def relay_h(c):
        return pltpu.make_async_remote_copy(fr_buf.at[c, mine], fr_buf.at[c, mine], rs_sem.at[c], rr_sem.at[c], device_id={"dp": dp, "tp": tp_other}, device_id_type=MESH)

    def send_targets(k):
        to = tp if k == 0 else tp_other
        return pltpu.make_async_remote_copy(tg_send, tg_recv.at[core], ts_sem.at[k], tr_sem.at[core], device_id={"dp": dp_far, "tp": to}, device_id_type=MESH)

    fetch_x().start()
    for c in range(n_chunks):
        fetch_single(c).start()
    for c in range(first_single):
        fetch_shared(c).start()

    barrier = pltpu.get_barrier_semaphore()
    group = [(dp, k) for k in range(1, n_tp)] + [(dp_y, k) for k in range(n_tp)] + [(dp_z, k) for k in range(n_tp)]
    for d, k in group:
        pl.semaphore_signal(barrier, inc=1, device_id={"dp": d, "tp": (tp + k) % n_tp}, device_id_type=MESH)
    tg_send[...] = jnp.broadcast_to(tgt_ref[...].astype(jnp.float32), tg_send.shape)

    def clear(i, carry):
        z_buf[pl.ds(pl.multiple_of(i * 64, 64), 64), :] = jnp.zeros((64, 2 * tokens), jnp.float32)
        return carry

    lax.fori_loop(0, SHARED // 64, clear, 0)
    zs_buf[...] = jnp.zeros_like(zs_buf)

    fetch_x().wait()

    def norm_rows(row):
        sl = pl.ds(pl.multiple_of(row, 16), 16)
        x = x_buf[sl, :].astype(jnp.float32)
        mean = jnp.mean(x, axis=-1, keepdims=True)
        c = x - mean
        var = jnp.mean(c * c, axis=-1, keepdims=True)
        h = (c * lax.rsqrt(var + LN_EPS) * gain_ref[...] + bias_ref[...]).astype(jnp.bfloat16)
        for k in range(n_chunks):
            h_buf[k, sl, :] = h[:, k * CHUNK:(k + 1) * CHUNK]
        return h

    def norm_sent(g, carry):
        h = norm_rows(core * half + g * 16).astype(jnp.float32)
        for k in range(n_chunks):
            hs_buf[k, pl.ds(pl.multiple_of(g * 16, 16), 16), :] = h[:, k * CHUNK:(k + 1) * CHUNK]
        return carry

    def norm_kept(g, carry):
        norm_rows((1 - core) * half + g * 16)
        return carry

    lax.fori_loop(0, half // 16, norm_sent, 0)
    pl.semaphore_wait(barrier, len(group))
    for c in range(n_chunks):
        send_h(c).start()
    for k in range(2):
        send_targets(k).start()
    lax.fori_loop(0, half // 16, norm_kept, 0)

    def single_chunk(c, carry):
        fetch_single(c).wait()
        zs_buf[...] += lax.dot_general(single_ref(c)[...], h_buf[c, 0:tokens, :], NT, preferred_element_type=jnp.float32)
        return carry

    lax.fori_loop(0, n_chunks, single_chunk, 0)
    for c in range(first_single, n_chunks):
        fetch_shared(c).start()

    def row_ids(block, start):
        shape = (block // 8, 8, 1)
        return lax.broadcasted_iota(jnp.int32, shape, 0) * 8 + lax.broadcasted_iota(jnp.int32, shape, 1) + start

    def stats(z_ref, n_rows, block, start, target, limit):
        lanes = z_ref.shape[1]

        def load(i):
            zz = z_ref[pl.ds(pl.multiple_of(i * block, block), block), :].reshape(block // 8, 8, lanes)
            ids = row_ids(block, start + i * block)
            if limit is not None:
                zz = jnp.where(ids < limit, zz, NEG_INF)
            return zz, ids

        def top(i, carry):
            m8, t8 = carry
            zz, ids = load(i)
            return jnp.maximum(m8, jnp.max(zz, axis=0)), t8 + jnp.sum(jnp.where(ids == target[None], zz, 0.0), axis=0)

        m8, t8 = lax.fori_loop(0, n_rows // block, top, (jnp.full((8, lanes), NEG_INF), jnp.zeros((8, lanes), jnp.float32)))
        m1 = jnp.max(m8, axis=0, keepdims=True)

        def add(i, s8):
            zz, _ = load(i)
            return s8 + jnp.sum(jnp.exp(zz - m1[None]), axis=0)

        s8 = lax.fori_loop(0, n_rows // block, add, jnp.zeros((8, lanes), jnp.float32))
        return m1, jnp.sum(s8, axis=0, keepdims=True), jnp.sum(t8, axis=0, keepdims=True)

    target = tgt_ref[...]
    m_s, s_s, t_s = stats(zs_buf, single, 128, first_row + 2 * SHARED, target, OPT_VOCAB)

    send_h(0).wait_recv()
    relay_h(0).start()

    def shared_chunk(c, carry):
        @pl.when(c + 1 < n_chunks)
        def _():
            send_h(c + 1).wait_recv()
            relay_h(c + 1).start()
        relay_h(c).wait_recv()
        h_buf[c, tokens:2 * tokens, :] = fr_buf[c].astype(jnp.bfloat16)
        fetch_shared(c).wait()
        z_buf[...] += lax.dot_general(e_buf[c], h_buf[c], NT, preferred_element_type=jnp.float32)
        return carry

    lax.fori_loop(0, n_chunks, shared_chunk, 0)

    for k in range(2):
        pltpu.make_async_remote_copy(tg_send, tg_recv.at[k], ts_sem.at[k], tr_sem.at[k], device_id={"dp": dp_far, "tp": tp}, device_id_type=MESH).wait_recv()
    lane = lax.broadcasted_iota(jnp.int32, (1, tokens), 1)
    far_target = jnp.where(lane < half, tg_recv[0, 0:1, :], tg_recv[1, 0:1, :]).astype(jnp.int32)
    both = jnp.concatenate([target, far_target], axis=1)
    m_h, s_h, t_h = stats(z_buf, SHARED, 128, first_row + shared_row, both, None)

    m_o = jnp.maximum(m_s, m_h[:, :tokens])
    s_o = s_s * jnp.exp(m_s - m_o) + s_h[:, :tokens] * jnp.exp(m_h[:, :tokens] - m_o)
    t_o = t_s + t_h[:, :tokens]
    own_send[0:1, :] = m_o
    own_send[1:2, :] = s_o
    own_send[2:3, :] = t_o
    far_send[0:1, :] = m_h[:, tokens:]
    far_send[1:2, :] = s_h[:, tokens:]
    far_send[2:3, :] = t_h[:, tokens:]

    copies = []
    for i, (d, k) in enumerate(group):
        src = own_send if i < n_tp - 1 else far_send
        dst = own_recv.at[k - 1] if i < n_tp - 1 else (y_recv.at[k] if i < 2 * n_tp - 1 else z_recv.at[k])
        copies.append(pltpu.make_async_remote_copy(src, dst, ss_sem.at[i], sr_sem.at[i], device_id={"dp": d, "tp": (tp + k) % n_tp}, device_id_type=MESH))
    for c in copies:
        c.start()
    for c in range(n_chunks):
        send_h(c).wait_send()
        relay_h(c).wait_send()
    for k in range(2):
        send_targets(k).wait_send()
    for c in copies:
        c.wait_recv()

    parts = [(m_o, s_o, t_o)]
    for k in range(n_tp - 1):
        parts.append(tuple(own_recv[k, j:j + 1, :] for j in range(3)))
    for k in range(n_tp):
        parts.append(tuple(jnp.where(lane < half, y_recv[k, j:j + 1, :], z_recv[k, j:j + 1, :]) for j in range(3)))
    m = functools.reduce(jnp.maximum, [p[0] for p in parts])
    total = sum(p[1] * jnp.exp(p[0] - m) for p in parts)
    z_t = sum(p[2] for p in parts)
    norm = m + jnp.log(total)
    logp = (z_t - norm) * msk_ref[...].astype(jnp.float32)
    out_ref[0:1, :] = norm
    out_ref[1:2, :] = logp
    out_ref[2:3, :] = m - norm
    out_ref[3:4, :] = jnp.broadcast_to(jnp.sum(logp, axis=-1, keepdims=True), logp.shape)
    for c in copies:
        c.wait_send()


def solution(mesh):
    n_tp = mesh.shape["tp"]

    def local_part(hidden, ln_gain, ln_bias, embedding, targets, score_mask):
        _, tokens, width = hidden.shape
        rows = embedding.shape[0]
        n_chunks = width // CHUNK
        single = rows - 2 * SHARED
        vmem = pl.BlockSpec(memory_space=pltpu.VMEM)
        hbm = pl.BlockSpec(memory_space=pl.ANY)
        f32, bf16 = jnp.float32, jnp.bfloat16
        dma = pltpu.SemaphoreType.DMA
        n_group = 3 * n_tp - 1
        out = pl.pallas_call(
            functools.partial(kernel, n_tp),
            out_shape=jax.ShapeDtypeStruct((8, tokens), f32),
            in_specs=[hbm, vmem, vmem, hbm, vmem, vmem],
            out_specs=vmem,
            scratch_shapes=[
                pltpu.VMEM((tokens, width), bf16),
                pltpu.VMEM((n_chunks, 2 * tokens, CHUNK), bf16),
                pltpu.VMEM((n_chunks, tokens // 2, CHUNK), f32),
                pltpu.VMEM((n_chunks, tokens, CHUNK), f32),
                pltpu.VMEM((n_chunks, SHARED, CHUNK), bf16),
                pltpu.VMEM((SHARED, 2 * tokens), f32),
                pltpu.VMEM((single, tokens), f32),
                pltpu.VMEM((8, tokens), f32),
                pltpu.VMEM((2, 8, tokens), f32),
                pltpu.VMEM((8, tokens), f32),
                pltpu.VMEM((8, tokens), f32),
                pltpu.VMEM((n_tp - 1, 8, tokens), f32),
                pltpu.VMEM((n_tp, 8, tokens), f32),
                pltpu.VMEM((n_tp, 8, tokens), f32),
                dma, dma((n_chunks,)), dma((n_chunks,)), dma((n_chunks,)), dma((n_chunks,)), dma((n_chunks,)), dma((n_chunks,)),
                dma((2,)), dma((2,)), dma((n_group,)), dma((n_group,)),
            ],
            compiler_params=pltpu.CompilerParams(collective_id=0, has_side_effects=True, vmem_limit_bytes=67043328),
        )(hidden, ln_gain.reshape(1, width), ln_bias.reshape(1, width), embedding, targets, score_mask)
        return out[0:1], out[1:2], out[3, :1], out[2:3]

    row_spec = P("dp", None)
    return jax.shard_map(local_part, mesh=mesh, in_specs=(P("dp", None, None), P(), P(), P("tp", None), row_spec, row_spec), out_specs=(row_spec, row_spec, P("dp"), row_spec), check_vma=False)
```

time: 69.7 us -> 49.1 us (0.70)
  Pallas kernels: 0 us -> 45.7 us
  matrix products: 44.8 us -> 0 us
  blocking collectives: 14.4 us -> 0 us
  other arithmetic: 9.41 us -> 0 us
  local copies, waits for them, and re-layouts: 0.01 us -> 2.49 us
    pallas_call x0 -> x1, Pallas kernels: none -> 45.7 us  [local_part(): pl.pallas_call(functools.partial(kernel, n_tp), out_shape=jax.ShapeDtypeS...]
    dot_general x1 -> x0, matrix products: 44.8 us -> none  [local_part(): jnp.einsum('bsd,vd->bsv', normed, embedding, preferred_element_type=jnp.f...]
    reduce_sum x4 -> x0, other arithmetic: 8.84 us -> none  [the longest x1 4.62 us: local_part(): exp_sum = jnp.sum(jnp.exp(logits - row_max[..., None]), axis=-1)]
    pmax x1 -> x0, blocking collectives: 8.61 us -> none  [local_part(): row_max = lax.pmax(jnp.max(logits, axis=-1), 'tp')]
    psum x1 -> x0, blocking collectives: 5.76 us -> none  [local_part(): combined = lax.psum(jnp.stack([exp_sum, target_part]), 'tp')]
    slice x0 -> x2, local copies, waits for them, and re-layouts: none -> 2.49 us  [local_part(): return (out[0:1], out[1:2], out[3, :1], out[2:3])]
where the time goes in v2:
time: 49.1 us; the launch traced here: 48.8 us
  Pallas kernels  45.7 us (93%)
  local copies, waits for them, and re-layouts  2.49 us (5%)
  between operations  0.64 us (1%)
    pallas_call x1, Pallas kernels, local_part(): pl.pallas_call(functools.partial(kernel, n_tp), out_shape=jax.ShapeDtypeS...  45.7 us
    slice x2, local copies, waits for them, and re-layouts, local_part(): return (out[0:1], out[1:2], out[3, :1], out[2:3])  2.49 us

profile of v2, /device:TPU:0, one launch (start us, length us, event | category | flops | bytes accessed | tf_op | source)
XLA Modules:
  0.0 48.8 jit_solution(17482403431917985447)
XLA Ops:
  0.6 45.7 %shard_map.93 = f32[8,128]{1,0:T(8,128)} custom-call(bf16[1,128,4096]{2,1,0:T(8,128)(2,1)} %x_hbm.1, f32[1,4096]{1,0:T(1,128)} %bitcast.3, f32[1,4096]{1,0:T(1,128)} %bitcast.4, bf16[12672,4096]{1,0:T(8,128)(2,1)} %emb_hbm.1, s32[1,128]{1,0:T(1,128)} %tgt_ref.1, s32[1,128]{1,0:T(1,128)} %msk_ref.1), custom_call_target="tpu_custom_call" | custom-call | tf_op jit(solution)/shard_map/pallas_call | solution.py:233
  46.4 1.3 %fusion = (f32[1,128]{1,0:T(1,128)}, f32[1,128]{1,0:T(1,128)}, f32[1,128]{1,0:T(1,128)}) fusion(f32[8,128]{1,0:T(8,128)} %shard_map.93), kind=kLoop, calls=%fused_computation | loop fusion | bytes 3072 | tf_op jit(solution)/shard_map/slice | solution.py:258
  47.7 1.2 %slice.14 = f32[1,1]{1,0:T(1,128)} slice(f32[8,128]{1,0:T(8,128)} %shard_map.93), slice={[3:4], [0:1]} | slice | bytes 8 | tf_op jit(solution)/shard_map/slice | solution.py:258

commit v3 on v2

v3 whole, which is shorter than its diff:
```python
import functools

import jax
import jax.numpy as jnp
from jax import lax
from jax.experimental import pallas as pl
from jax.experimental.pallas import tpu as pltpu
from jax.sharding import PartitionSpec as P

OPT_VOCAB = 50272
LN_EPS = 1e-5
CHUNK = 512
SHARED = 5632
BLOCK = 704
MESH = pl.DeviceIdType.MESH
NEG_INF = float("-inf")
NT = (((1,), (1,)), ((), ()))


def kernel(n_tp, x_hbm, gain_hbm, bias_hbm, emb_hbm, tgt_hbm, msk_hbm, out_ref,
           gain_ref, bias_ref, tgt_ref, msk_ref, x_buf, h_buf, hs_buf, fr_buf, e_buf, z_buf, zs_buf, tg_send, tg_recv, own_send, far_send, own_recv, y_recv, z_recv,
           in_sem, x_sem, s_sem, e_sem, hs_sem, hr_sem, rs_sem, rr_sem, ts_sem, tr_sem, ss_sem, sr_sem):
    dp, tp = lax.axis_index("dp"), lax.axis_index("tp")
    rows, width = emb_hbm.shape
    tokens = x_buf.shape[0]
    half = tokens // 2
    n_slots = width // CHUNK
    last = n_slots
    short = CHUNK // 2
    single = rows - 2 * SHARED
    per_slot = SHARED // single
    first_single = n_slots - pl.cdiv(n_slots, per_slot)
    core, y, z = tp % 2, dp % 2, dp // 2
    parity = (y + z) % 2
    dp_y, dp_z = dp + 1 - 2 * y, dp + 2 - 4 * z
    dp_far = dp_y + core * (dp_z - dp_y)
    tp_other = tp + 1 - 2 * core
    first_row = tp * rows
    shared_row = pl.multiple_of(parity * SHARED, 16)
    mine = pl.ds(pl.multiple_of(core * half, half), half)

    def place(c):
        if isinstance(c, int) and c in (0, last):
            return 0, pl.ds(0 if c == 0 else short, short), pl.ds(0 if c == 0 else width - short, short)
        start = c * CHUNK - short
        return c, pl.ds(0, CHUNK), pl.ds(start if isinstance(c, int) else pl.multiple_of(start, short), CHUNK)

    def fetch_x():
        return pltpu.make_async_copy(x_hbm.at[0], x_buf, x_sem)

    def single_at(slot):
        return first_single + slot // per_slot, pl.ds(pl.multiple_of(slot % per_slot * single, 16), single)

    def fetch_single(c):
        slot, lanes, cols = place(c)
        at, sl = single_at(slot)
        return pltpu.make_async_copy(emb_hbm.at[pl.ds(2 * SHARED, single), cols], e_buf.at[at, sl, lanes], s_sem.at[c])

    def fetch_shared(c):
        slot, lanes, cols = place(c)
        return pltpu.make_async_copy(emb_hbm.at[pl.ds(shared_row, SHARED), cols], e_buf.at[slot, :, lanes], e_sem.at[c])

    def send_h(c):
        slot, lanes, _ = place(c)
        return pltpu.make_async_remote_copy(hs_buf.at[slot, :, lanes], fr_buf.at[slot, mine, lanes], hs_sem.at[c], hr_sem.at[c], device_id={"dp": dp_far, "tp": tp}, device_id_type=MESH)

    def relay_h(c):
        slot, lanes, _ = place(c)
        ref = fr_buf.at[slot, mine, lanes]
        return pltpu.make_async_remote_copy(ref, ref, rs_sem.at[c], rr_sem.at[c], device_id={"dp": dp, "tp": tp_other}, device_id_type=MESH)

    def send_targets(k):
        to = tp if k == 0 else tp_other
        return pltpu.make_async_remote_copy(tg_send, tg_recv.at[core], ts_sem.at[k], tr_sem.at[core], device_id={"dp": dp_far, "tp": to}, device_id_type=MESH)

    small = [pltpu.make_async_copy(src, dst, in_sem.at[i]) for i, (src, dst) in enumerate(
        [(tgt_hbm, tgt_ref), (gain_hbm, gain_ref), (bias_hbm, bias_ref), (msk_hbm, msk_ref)])]
    fetch_x().start()
    for c in small:
        c.start()
    for c in range(4):
        fetch_single(c).start()

    barrier = pltpu.get_barrier_semaphore()
    group = [(dp, k) for k in range(1, n_tp)] + [(dp_y, k) for k in range(n_tp)] + [(dp_z, k) for k in range(n_tp)]
    for d, k in group:
        pl.semaphore_signal(barrier, inc=1, device_id={"dp": d, "tp": (tp + k) % n_tp}, device_id_type=MESH)
    for c in small:
        c.wait()
    tg_send[...] = jnp.broadcast_to(tgt_ref[...].astype(jnp.float32), tg_send.shape)

    fetch_x().wait()
    for c in range(4, last + 1):
        fetch_single(c).start()

    def norm_rows(row):
        sl = pl.ds(pl.multiple_of(row, 16), 16)
        x = x_buf[sl, :].astype(jnp.float32)
        mean = jnp.mean(x, axis=-1, keepdims=True)
        c = x - mean
        var = jnp.mean(c * c, axis=-1, keepdims=True)
        h = (c * lax.rsqrt(var + LN_EPS) * gain_ref[...] + bias_ref[...]).astype(jnp.bfloat16)
        for k in range(last + 1):
            slot, lanes, cols = place(k)
            h_buf[slot, sl, lanes] = h[:, cols.start:cols.start + cols.size]
        return h

    def norm_sent(g, carry):
        h = norm_rows(core * half + g * 16).astype(jnp.float32)
        for k in range(last + 1):
            slot, lanes, cols = place(k)
            hs_buf[slot, pl.ds(pl.multiple_of(g * 16, 16), 16), lanes] = h[:, cols.start:cols.start + cols.size]
        return carry

    def norm_kept(g, carry):
        norm_rows((1 - core) * half + g * 16)
        return carry

    lax.fori_loop(0, half // 16, norm_sent, 0)
    fetch_shared(0).start()
    pl.semaphore_wait(barrier, len(group))
    for c in range(last + 1):
        send_h(c).start()
    for k in range(2):
        send_targets(k).start()
    lax.fori_loop(0, half // 16, norm_kept, 0)

    def single_dot(c):
        slot, lanes, _ = place(c)
        at, sl = single_at(slot)
        return lax.dot_general(e_buf[at, sl, lanes], h_buf[slot, 0:tokens, lanes], NT, preferred_element_type=jnp.float32)

    def single_chunk(c, carry):
        fetch_single(c).wait()

        @pl.when(c == 4)
        def _():
            fetch_shared(1).start()
        zs_buf[...] += single_dot(c)
        return carry

    fetch_single(0).wait()
    zs_buf[...] = single_dot(0)
    lax.fori_loop(1, last, single_chunk, 0)
    fetch_single(last).wait()
    zs_buf[...] += single_dot(last)

    sub = lax.broadcasted_iota(jnp.int32, (8, 1), 0)
    lane = lax.broadcasted_iota(jnp.int32, (1, tokens), 1)

    def online(z, start, target, state, limit=None):
        n_rows, lanes = z.shape
        z = z.reshape(n_rows // 8, 8, lanes)
        step = lax.broadcasted_iota(jnp.int32, z.shape, 0) * 8
        if limit is not None:
            z = jnp.where(step < (limit - start) - sub[None], z, NEG_INF)
        t8 = jnp.sum(jnp.where(step == (target - start - sub)[None], z, 0.0), axis=0)
        m8 = jnp.max(z, axis=0)
        if state is None:
            return m8, jnp.sum(jnp.exp(z - m8[None]), axis=0), t8
        m_new = jnp.maximum(state[0], m8)
        s8 = state[1] * jnp.exp(state[0] - m_new) + jnp.sum(jnp.exp(z - m_new[None]), axis=0)
        return m_new, s8, state[2] + t8

    def fold(state):
        m1 = jnp.max(state[0], axis=0, keepdims=True)
        return m1, jnp.sum(state[1] * jnp.exp(state[0] - m1), axis=0, keepdims=True), jnp.sum(state[2], axis=0, keepdims=True)

    send_h(0).wait_recv()
    relay_h(0).start()

    def shared_ready(c):
        fetch_shared(c).wait()
        if isinstance(c, int):
            if c + 1 <= last:
                send_h(c + 1).wait_recv()
                relay_h(c + 1).start()
            if c + 2 <= last:
                fetch_shared(c + 2).start()
        else:
            @pl.when(c + 1 < last)
            def _():
                send_h(c + 1).wait_recv()
                relay_h(c + 1).start()

            @pl.when(c + 1 == last)
            def _():
                send_h(last).wait_recv()
                relay_h(last).start()

            @pl.when(c + 2 < last)
            def _():
                fetch_shared(c + 2).start()

            @pl.when(c + 2 == last)
            def _():
                fetch_shared(last).start()
        relay_h(c).wait_recv()
        slot, lanes, _ = place(c)
        h_buf[slot, tokens:2 * tokens, lanes] = fr_buf[slot, :, lanes].astype(jnp.bfloat16)

    def shared_dot(c, sl):
        slot, lanes, _ = place(c)
        return lax.dot_general(e_buf[slot, sl, lanes], h_buf[slot, :, lanes], NT, preferred_element_type=jnp.float32)

    target = tgt_ref[...]
    every = pl.ds(0, SHARED)
    shared_ready(0)
    z_buf[...] = shared_dot(0, every)
    m_s, s_s, t_s = fold(online(zs_buf[...], first_row + 2 * SHARED, target, None, OPT_VOCAB))

    def shared_chunk(c, carry):
        shared_ready(c)
        z_buf[...] += shared_dot(c, every)
        return carry

    lax.fori_loop(1, last, shared_chunk, 0)

    for k in range(2):
        pltpu.make_async_remote_copy(tg_send, tg_recv.at[k], ts_sem.at[k], tr_sem.at[k], device_id={"dp": dp_far, "tp": tp}, device_id_type=MESH).wait_recv()
    far_target = jnp.where(lane < half, tg_recv[0, 0:1, :], tg_recv[1, 0:1, :]).astype(jnp.int32)
    both = jnp.concatenate([target, far_target], axis=1)
    shared_ready(last)

    def rows_of(i):
        return pl.ds(pl.multiple_of(i * BLOCK, BLOCK), BLOCK)

    def step(i, state):
        state = online(z_buf[rows_of(i), :], first_row + shared_row + i * BLOCK, both, state)

        if not isinstance(i, int):
            sl = rows_of(i + 1)
            z_buf[sl, :] += shared_dot(last, sl)
        return state

    z_buf[rows_of(0), :] += shared_dot(last, rows_of(0))
    n_blocks = SHARED // BLOCK
    empty = (jnp.full((8, 2 * tokens), NEG_INF), jnp.zeros((8, 2 * tokens), jnp.float32), jnp.zeros((8, 2 * tokens), jnp.float32))
    m_h, s_h, t_h = fold(step(n_blocks - 1, lax.fori_loop(0, n_blocks - 1, step, empty)))

    m_o = jnp.maximum(m_s, m_h[:, :tokens])
    s_o = s_s * jnp.exp(m_s - m_o) + s_h[:, :tokens] * jnp.exp(m_h[:, :tokens] - m_o)
    t_o = t_s + t_h[:, :tokens]
    own_send[0:1, :] = m_o
    own_send[1:2, :] = s_o
    own_send[2:3, :] = t_o
    far_send[0:1, :] = m_h[:, tokens:]
    far_send[1:2, :] = s_h[:, tokens:]
    far_send[2:3, :] = t_h[:, tokens:]

    copies = []
    for i, (d, k) in enumerate(group):
        src = own_send if i < n_tp - 1 else far_send
        dst = own_recv.at[k - 1] if i < n_tp - 1 else (y_recv.at[k] if i < 2 * n_tp - 1 else z_recv.at[k])
        copies.append(pltpu.make_async_remote_copy(src, dst, ss_sem.at[i], sr_sem.at[i], device_id={"dp": d, "tp": (tp + k) % n_tp}, device_id_type=MESH))
    for c in copies:
        c.start()
    for c in range(last + 1):
        send_h(c).wait_send()
        relay_h(c).wait_send()
    for k in range(2):
        send_targets(k).wait_send()
    for c in copies:
        c.wait_recv()

    parts = [(m_o, s_o, t_o)]
    for k in range(n_tp - 1):
        parts.append(tuple(own_recv[k, j:j + 1, :] for j in range(3)))
    for k in range(n_tp):
        parts.append(tuple(jnp.where(lane < half, y_recv[k, j:j + 1, :], z_recv[k, j:j + 1, :]) for j in range(3)))
    m = functools.reduce(jnp.maximum, [p[0] for p in parts])
    total = sum(p[1] * jnp.exp(p[0] - m) for p in parts)
    z_t = sum(p[2] for p in parts)
    norm = m + jnp.log(total)
    logp = (z_t - norm) * msk_ref[...].astype(jnp.float32)
    out_ref[0:1, :] = norm
    out_ref[1:2, :] = logp
    out_ref[2:3, :] = m - norm
    for c in copies:
        c.wait_send()


def finish(all_ref, norm_ref, logp_ref, seq_ref, top_ref):
    logp = all_ref[1:2, :]
    norm_ref[...] = all_ref[0:1, :]
    logp_ref[...] = logp
    top_ref[...] = all_ref[2:3, :]
    seq_ref[...] = jnp.sum(logp, axis=-1, keepdims=True)


def solution(mesh):
    n_tp = mesh.shape["tp"]

    def local_part(hidden, ln_gain, ln_bias, embedding, targets, score_mask):
        _, tokens, width = hidden.shape
        rows = embedding.shape[0]
        n_slots = width // CHUNK
        single = rows - 2 * SHARED
        vmem = pl.BlockSpec(memory_space=pltpu.VMEM)
        hbm = pl.BlockSpec(memory_space=pl.ANY)
        f32, bf16 = jnp.float32, jnp.bfloat16
        dma = pltpu.SemaphoreType.DMA
        n_group = 3 * n_tp - 1
        out = pl.pallas_call(
            functools.partial(kernel, n_tp),
            out_shape=jax.ShapeDtypeStruct((8, tokens), f32),
            in_specs=[hbm] * 6,
            out_specs=vmem,
            scratch_shapes=[
                pltpu.VMEM((1, width), f32),
                pltpu.VMEM((1, width), f32),
                pltpu.VMEM((1, tokens), jnp.int32),
                pltpu.VMEM((1, tokens), jnp.int32),
                pltpu.VMEM((tokens, width), bf16),
                pltpu.VMEM((n_slots, 2 * tokens, CHUNK), bf16),
                pltpu.VMEM((n_slots, tokens // 2, CHUNK), f32),
                pltpu.VMEM((n_slots, tokens, CHUNK), f32),
                pltpu.VMEM((n_slots, SHARED, CHUNK), bf16),
                pltpu.VMEM((SHARED, 2 * tokens), f32),
                pltpu.VMEM((single, tokens), f32),
                pltpu.VMEM((8, tokens), f32),
                pltpu.VMEM((2, 8, tokens), f32),
                pltpu.VMEM((8, tokens), f32),
                pltpu.VMEM((8, tokens), f32),
                pltpu.VMEM((n_tp - 1, 8, tokens), f32),
                pltpu.VMEM((n_tp, 8, tokens), f32),
                pltpu.VMEM((n_tp, 8, tokens), f32),
                dma((4,)), dma, *[dma((n_slots + 1,))] * 6,
                dma((2,)), dma((2,)), dma((n_group,)), dma((n_group,)),
            ],
            compiler_params=pltpu.CompilerParams(collective_id=0, has_side_effects=True, vmem_limit_bytes=67043328),
        )(hidden, ln_gain.reshape(1, width), ln_bias.reshape(1, width), embedding, targets, score_mask)
        row = jax.ShapeDtypeStruct((1, tokens), f32)
        norm, logp, seq, top = pl.pallas_call(
            finish, out_shape=(row, row, jax.ShapeDtypeStruct((1, 1), f32), row), in_specs=[vmem], out_specs=(vmem,) * 4,
        )(out)
        return norm, logp, seq.reshape(1), top

    row_spec = P("dp", None)
    return jax.shard_map(local_part, mesh=mesh, in_specs=(P("dp", None, None), P(), P(), P("tp", None), row_spec, row_spec), out_specs=(row_spec, row_spec, P("dp"), row_spec), check_vma=False)
```

time: 49.1 us -> 35.8 us (0.73)
  Pallas kernels: 45.7 us -> 34.9 us
  local copies, waits for them, and re-layouts: 2.49 us -> 0 us
    pallas_call x1, Pallas kernels: 45.7 us -> 33.7 us  [local_part(): pl.pallas_call(functools.partial(kernel, n_tp), out_shape=jax.ShapeDtypeS...]
    slice x2 -> x0, local copies, waits for them, and re-layouts: 2.49 us -> none  [local_part(): return (out[0:1], out[1:2], out[3, :1], out[2:3])]
    pallas_call x0 -> x1, Pallas kernels: none -> 1.26 us  [local_part(): pl.pallas_call(finish, out_shape=(row, row, jax.ShapeDtypeStruct((1, 1),...]
where the time goes in v3:
time: 35.8 us; the launch traced here: 35.6 us
  Pallas kernels  34.9 us (97%)
  between operations  0.64 us (2%)
    pallas_call x1, Pallas kernels, local_part(): pl.pallas_call(functools.partial(kernel, n_tp), out_shape=jax.ShapeDtypeS...  33.7 us
    pallas_call x1, Pallas kernels, local_part(): pl.pallas_call(finish, out_shape=(row, row, jax.ShapeDtypeStruct((1, 1),...  1.26 us

profile of v3, /device:TPU:0, one launch (start us, length us, event | category | flops | bytes accessed | tf_op | source)
XLA Modules:
  0.0 35.6 jit_solution(13470528639556566995)
XLA Ops:
  0.6 33.7 %shard_map.93.all_ref = f32[8,128]{1,0:T(8,128)} custom-call(bf16[1,128,4096]{2,1,0:T(8,128)(2,1)} %x_hbm.1, f32[1,4096]{1,0:T(1,128)} %bitcast.3, f32[1,4096]{1,0:T(1,128)} %bitcast.4, bf16[12672,4096]{1,0:T(8,128)(2,1)} %emb_hbm.1, s32[1,128]{1,0:T(1,128)} %tgt_hbm.1, s32[1,128]{1,0:T(1,128)} %msk_hbm.1), custom_call_target="tpu_custom_call" | custom-call | tf_op jit(solution)/shard_map/pallas_call | solution.py:304
  34.3 1.3 %shard_map.94 = (f32[1,128]{1,0:T(1,128)}, f32[1,128]{1,0:T(1,128)}, f32[1,1]{1,0:T(1,128)}, f32[1,128]{1,0:T(1,128)}) custom-call(f32[8,128]{1,0:T(8,128)} %shard_map.93.all_ref), custom_call_target="tpu_custom_call" | custom-call | tf_op jit(solution)/shard_map/pallas_call | solution.py:334

commit v4 on v3

--- a/solution.py
+++ b/solution.py
@@ -79,7 +79,7 @@
     for c in small:
         c.start()
     for c in range(4):
-        fetch_single(c).start()
+        fetch_single(c).start(priority=1)
 
     barrier = pltpu.get_barrier_semaphore()
     group = [(dp, k) for k in range(1, n_tp)] + [(dp_y, k) for k in range(n_tp)] + [(dp_z, k) for k in range(n_tp)]
@@ -91,7 +91,7 @@
 
     fetch_x().wait()
     for c in range(4, last + 1):
-        fetch_single(c).start()
+        fetch_single(c).start(priority=1)
 
     def norm_rows(row):
         sl = pl.ds(pl.multiple_of(row, 16), 16)
@@ -117,7 +117,7 @@
         return carry
 
     lax.fori_loop(0, half // 16, norm_sent, 0)
-    fetch_shared(0).start()
+    fetch_shared(0).start(priority=1)
     pl.semaphore_wait(barrier, len(group))
     for c in range(last + 1):
         send_h(c).start()
@@ -135,13 +135,15 @@
 
         @pl.when(c == 4)
         def _():
-            fetch_shared(1).start()
+            fetch_shared(1).start(priority=1)
         zs_buf[...] += single_dot(c)
         return carry
 
     fetch_single(0).wait()
     zs_buf[...] = single_dot(0)
     lax.fori_loop(1, last, single_chunk, 0)
+    send_h(0).wait_recv()
+    relay_h(0).start()
     fetch_single(last).wait()
     zs_buf[...] += single_dot(last)
 
@@ -166,9 +168,6 @@
         m1 = jnp.max(state[0], axis=0, keepdims=True)
         return m1, jnp.sum(state[1] * jnp.exp(state[0] - m1), axis=0, keepdims=True), jnp.sum(state[2], axis=0, keepdims=True)
 
-    send_h(0).wait_recv()
-    relay_h(0).start()
-
     def shared_ready(c):
         fetch_shared(c).wait()
         if isinstance(c, int):
@@ -176,7 +175,7 @@
                 send_h(c + 1).wait_recv()
                 relay_h(c + 1).start()
             if c + 2 <= last:
-                fetch_shared(c + 2).start()
+                fetch_shared(c + 2).start(priority=1)
         else:
             @pl.when(c + 1 < last)
             def _():
@@ -190,11 +189,11 @@
 
             @pl.when(c + 2 < last)
             def _():
-                fetch_shared(c + 2).start()
+                fetch_shared(c + 2).start(priority=1)
 
             @pl.when(c + 2 == last)
             def _():
-                fetch_shared(last).start()
+                fetch_shared(last).start(priority=1)
         relay_h(c).wait_recv()
         slot, lanes, _ = place(c)
         h_buf[slot, tokens:2 * tokens, lanes] = fr_buf[slot, :, lanes].astype(jnp.bfloat16)
@@ -303,7 +302,7 @@
         n_group = 3 * n_tp - 1
         out = pl.pallas_call(
             functools.partial(kernel, n_tp),
-            out_shape=jax.ShapeDtypeStruct((8, tokens), f32),
+            out_shape=pltpu.VMEM((8, tokens), f32),
             in_specs=[hbm] * 6,
             out_specs=vmem,
             scratch_shapes=[
@@ -328,12 +327,12 @@
                 dma((4,)), dma, *[dma((n_slots + 1,))] * 6,
                 dma((2,)), dma((2,)), dma((n_group,)), dma((n_group,)),
             ],
-            compiler_params=pltpu.CompilerParams(collective_id=0, has_side_effects=True, vmem_limit_bytes=67043328),
+            compiler_params=pltpu.CompilerParams(collective_id=0, has_side_effects=True, vmem_limit_bytes=63 << 20),
         )(hidden, ln_gain.reshape(1, width), ln_bias.reshape(1, width), embedding, targets, score_mask)
         row = jax.ShapeDtypeStruct((1, tokens), f32)
         norm, logp, seq, top = pl.pallas_call(
             finish, out_shape=(row, row, jax.ShapeDtypeStruct((1, 1), f32), row), in_specs=[vmem], out_specs=(vmem,) * 4,
-        )(out)
+        )(pltpu.with_memory_space_constraint(out, pltpu.VMEM))
         return norm, logp, seq.reshape(1), top
 
     row_spec = P("dp", None)

time: 35.8 us -> 32.9 us (0.919)
  Pallas kernels: 34.9 us -> 32.2 us
    pallas_call x1, Pallas kernels: 33.7 us -> 31.6 us  [local_part(): pl.pallas_call(functools.partial(kernel, n_tp), out_shape=pltpu.VMEM((8,...]
    pallas_call x1, Pallas kernels: 1.26 us -> 0.59 us  [local_part(): pl.pallas_call(finish, out_shape=(row, row, jax.ShapeDtypeStruct((1, 1),...]
where the time goes in v4:
time: 32.9 us; the launch traced here: 32.8 us
  Pallas kernels  32.2 us (98%)
  between operations  0.64 us (2%)
    pallas_call x1, Pallas kernels, local_part(): pl.pallas_call(functools.partial(kernel, n_tp), out_shape=pltpu.VMEM((8,...  31.6 us

profile of v4, /device:TPU:0, one launch (start us, length us, event | category | flops | bytes accessed | tf_op | source)
XLA Modules:
  0.0 32.8 jit_solution(9783717898988877278)
XLA Ops:
  0.6 31.6 %shard_map.93.all_ref = f32[8,128]{1,0:T(8,128)S(1)} custom-call(bf16[1,128,4096]{2,1,0:T(8,128)(2,1)} %x_hbm.1, f32[1,4096]{1,0:T(1,128)} %bitcast.3, f32[1,4096]{1,0:T(1,128)} %bitcast.4, bf16[12672,4096]{1,0:T(8,128)(2,1)} %emb_hbm.1, s32[1,128]{1,0:T(1,128)} %tgt_hbm.1, s32[1,128]{1,0:T(1,128)} %msk_hbm.1), custom_call_target="tpu_custom_call" | custom-call | tf_op jit(solution)/shard_map/pallas_call | solution.py:303
  32.2 0.6 %shard_map.94 = (f32[1,128]{1,0:T(1,128)}, f32[1,128]{1,0:T(1,128)}, f32[1,1]{1,0:T(1,128)}, f32[1,128]{1,0:T(1,128)}) custom-call(f32[8,128]{1,0:T(8,128)S(1)} %shard_map.93.all_ref), custom_call_target="tpu_custom_call" | custom-call | tf_op jit(solution)/shard_map/pallas_call | solution.py:333

commit v5 on v4

v5 whole, which is shorter than its diff:
```python
import functools

import jax
import jax.numpy as jnp
from jax import lax
from jax.experimental import pallas as pl
from jax.experimental.pallas import tpu as pltpu
from jax.sharding import PartitionSpec as P

OPT_VOCAB = 50272
LN_EPS = 1e-5
CHUNK = 512
SHARED = 5632
BLOCK = 352
HELD = 7
NORM_ROWS = 32
MESH = pl.DeviceIdType.MESH
NEG_INF = float("-inf")
NT = (((1,), (1,)), ((), ()))


def kernel(n_tp, x_hbm, gain_hbm, bias_hbm, emb_hbm, tgt_hbm, msk_hbm, out_ref,
           gain_ref, bias_ref, tgt_ref, msk_ref, x_buf, h_buf, hs_buf, fr_buf, e_buf, z_buf, zs_buf, tg_send, tg_recv, own_send, far_send, all_recv,
           in_sem, x_sem, s_sem, e_sem, hs_sem, hr_sem, rs_sem, rr_sem, ts_sem, tr_sem, ss_sem, sr_sem):
    dp, tp = lax.axis_index("dp"), lax.axis_index("tp")
    rows, width = emb_hbm.shape
    tokens = x_buf.shape[1]
    half = tokens // 2
    n_slots = width // CHUNK
    last = n_slots
    short = CHUNK // 2
    single = rows - 2 * SHARED
    per_slot = SHARED // single
    n_held = e_buf.shape[0]
    first_single = n_held - pl.cdiv(n_slots, per_slot)
    core, y, z = tp % 2, dp % 2, dp // 2
    parity = (y + z) % 2
    dp_y, dp_z = dp + 1 - 2 * y, dp + 2 - 4 * z
    dp_far = dp_y + core * (dp_z - dp_y)
    tp_other = tp + 1 - 2 * core
    first_row = tp * rows
    shared_row = pl.multiple_of(parity * SHARED, 16)
    mine = pl.ds(pl.multiple_of(core * half, half), half)
    rest = pl.ds(pl.multiple_of((1 - core) * half, half), half)

    def place(c):
        if isinstance(c, int) and c in (0, last):
            return 0, pl.ds(0 if c == 0 else short, short), pl.ds(0 if c == 0 else width - short, short)
        start = c * CHUNK - short
        return c, pl.ds(0, CHUNK), pl.ds(start if isinstance(c, int) else pl.multiple_of(start, short), CHUNK)

    def fetch_x(c, part, sl):
        slot, lanes, cols = place(c)
        return pltpu.make_async_copy(x_hbm.at[0, sl, cols], x_buf.at[slot, sl, lanes], x_sem.at[part])

    def wait_x(part, sl):
        ref = x_buf.at[:, sl]
        pltpu.make_async_copy(ref, ref, x_sem.at[part]).wait()

    def single_at(slot):
        return first_single + slot // per_slot, pl.ds(pl.multiple_of(slot % per_slot * single, 16), single)

    def fetch_single(c):
        slot, lanes, cols = place(c)
        at, sl = single_at(slot)
        return pltpu.make_async_copy(emb_hbm.at[pl.ds(2 * SHARED, single), cols], e_buf.at[at, sl, lanes], s_sem.at[slot])

    def wait_single(slot):
        at, sl = single_at(slot)
        ref = e_buf.at[at, sl]
        pltpu.make_async_copy(ref, ref, s_sem.at[slot]).wait()

    def held(c):
        return n_slots - n_held if isinstance(c, int) and n_held <= c < last else c

    def fetch_shared(c):
        slot, lanes, cols = place(c)
        return pltpu.make_async_copy(emb_hbm.at[pl.ds(shared_row, SHARED), cols], e_buf.at[held(slot), :, lanes], e_sem.at[c])

    def send_h(c):
        slot, lanes, _ = place(c)
        return pltpu.make_async_remote_copy(hs_buf.at[slot, :, lanes], fr_buf.at[slot, mine, lanes], hs_sem, hr_sem.at[c], device_id={"dp": dp_far, "tp": tp}, device_id_type=MESH)

    def relay_h(c):
        slot, lanes, _ = place(c)
        ref = fr_buf.at[slot, mine, lanes]
        return pltpu.make_async_remote_copy(ref, ref, rs_sem, rr_sem.at[c], device_id={"dp": dp, "tp": tp_other}, device_id_type=MESH)

    def send_targets(k):
        to = tp if k == 0 else tp_other
        return pltpu.make_async_remote_copy(tg_send, tg_recv.at[core], ts_sem, tr_sem, device_id={"dp": dp_far, "tp": to}, device_id_type=MESH)

    small = [pltpu.make_async_copy(src, dst, in_sem.at[i]) for i, (src, dst) in enumerate(
        [(tgt_hbm, tgt_ref), (gain_hbm, gain_ref), (bias_hbm, bias_ref), (msk_hbm, msk_ref)])]
    for part, sl in enumerate((mine, rest)):
        for c in range(last + 1):
            fetch_x(c, part, sl).start()
    for c in small:
        c.start()
    for c in (0, last, 1, 2, 3):
        fetch_single(c).start(priority=1)

    barrier = pltpu.get_barrier_semaphore()
    group = [(dp, k) for k in range(1, n_tp)] + [(dp_y, k) for k in range(n_tp)] + [(dp_z, k) for k in range(n_tp)]
    for d, k in group:
        pl.semaphore_signal(barrier, inc=1, device_id={"dp": d, "tp": (tp + k) % n_tp}, device_id_type=MESH)
    for c in small:
        c.wait()
    tg_send[...] = jnp.broadcast_to(tgt_ref[...].astype(jnp.float32), tg_send.shape)

    wait_x(0, mine)
    for c in range(4, last):
        fetch_single(c).start(priority=1)
    for c in range(2):
        fetch_shared(c).start(priority=1)

    def norm_rows(row):
        sl = pl.ds(pl.multiple_of(row, NORM_ROWS), NORM_ROWS)

        def load(k):
            return x_buf[k, sl, :].astype(jnp.float32)

        def cols(ref, k):
            if k == 0:
                return jnp.concatenate([ref[:, 0:short], ref[:, width - short:width]], axis=1)
            return ref[:, k * CHUNK - short:(k + 1) * CHUNK - short]

        mean = jnp.sum(sum(load(k) for k in range(n_slots)), axis=-1, keepdims=True) / width
        var = jnp.sum(sum((load(k) - mean) * (load(k) - mean) for k in range(n_slots)), axis=-1, keepdims=True) / width
        scale = lax.rsqrt(var + LN_EPS)
        for k in range(n_slots):
            h = ((load(k) - mean) * scale * cols(gain_ref, k) + cols(bias_ref, k)).astype(jnp.bfloat16)
            h_buf[k, sl, :] = h
            yield k, h

    def norm_sent(g, carry):
        for k, h in norm_rows(core * half + g * NORM_ROWS):
            hs_buf[k, pl.ds(pl.multiple_of(g * NORM_ROWS, NORM_ROWS), NORM_ROWS), :] = h.astype(jnp.float32)
        return carry

    def norm_kept(g, carry):
        for _ in norm_rows((1 - core) * half + g * NORM_ROWS):
            pass
        return carry

    lax.fori_loop(0, half // NORM_ROWS, norm_sent, 0)
    pl.semaphore_wait(barrier, len(group))
    for c in range(last + 1):
        send_h(c).start()
    for k in range(2):
        send_targets(k).start()
    wait_x(1, rest)
    lax.fori_loop(0, half // NORM_ROWS, norm_kept, 0)

    def single_dot(slot):
        at, sl = single_at(slot)
        return lax.dot_general(e_buf[at, sl, :], h_buf[slot, 0:tokens, :], NT, preferred_element_type=jnp.float32)

    zs_buf[...] = jnp.zeros_like(zs_buf)

    def single_step(i, carry):
        @pl.when(i == 2)
        def _():
            fetch_shared(2).start(priority=1)

        @pl.when(i == 3)
        def _():
            send_h(0).wait_recv()
            relay_h(0).start()
        for k in range(2):
            wait_single(2 * i + k)
        zs_buf[...] += single_dot(2 * i) + single_dot(2 * i + 1)
        return carry

    lax.fori_loop(0, n_slots // 2, single_step, 0)

    sub = lax.broadcasted_iota(jnp.int32, (8, 1), 0)
    lane = lax.broadcasted_iota(jnp.int32, (1, tokens), 1)

    def online(z, start, target, state, limit=None):
        n_rows, lanes = z.shape
        z = z.reshape(n_rows // 8, 8, lanes)
        step = lax.broadcasted_iota(jnp.int32, z.shape, 0) * 8
        if limit is not None:
            z = jnp.where(step < (limit - start) - sub[None], z, NEG_INF)
        t8 = jnp.sum(jnp.where(step == (target - start - sub)[None], z, 0.0), axis=0)
        m8 = jnp.max(z, axis=0)
        if state is None:
            return m8, jnp.sum(jnp.exp(z - m8[None]), axis=0), t8
        m_new = jnp.maximum(state[0], m8)
        s8 = state[1] * jnp.exp(state[0] - m_new) + jnp.sum(jnp.exp(z - m_new[None]), axis=0)
        return m_new, s8, state[2] + t8

    def fold(state):
        m1 = jnp.max(state[0], axis=0, keepdims=True)
        return m1, jnp.sum(state[1] * jnp.exp(state[0] - m1), axis=0, keepdims=True), jnp.sum(state[2], axis=0, keepdims=True)

    def shared_ready(c):
        fetch_shared(c).wait()
        if isinstance(c, int):
            if c + 2 <= last:
                send_h(c + 1).wait_recv()
                relay_h(c + 1).start()
            if c + 3 <= last:
                fetch_shared(c + 3).start(priority=1)
        else:
            @pl.when(c + 1 < last)
            def _():
                send_h(c + 1).wait_recv()
                relay_h(c + 1).start()

            @pl.when(c + 2 == last)
            def _():
                send_h(last).wait_recv()
                relay_h(last).start()

            @pl.when(c + 3 < n_held)
            def _():
                fetch_shared(c + 3).start(priority=1)

            for k in range(n_held, last + 1):
                @pl.when(c + 3 == k)
                def _():
                    fetch_shared(k).start(priority=1)
        relay_h(c).wait_recv()
        slot, lanes, _ = place(c)
        h_buf[slot, tokens:2 * tokens, lanes] = fr_buf[slot, :, lanes].astype(jnp.bfloat16)

    def shared_dot(c, sl):
        slot, lanes, _ = place(c)
        return lax.dot_general(e_buf[held(slot), sl, lanes], h_buf[slot, :, lanes], NT, preferred_element_type=jnp.float32)

    target = tgt_ref[...]
    every = pl.ds(0, SHARED)
    shared_ready(0)
    z_buf[...] = shared_dot(0, every)
    m_s, s_s, t_s = fold(online(zs_buf[...], first_row + 2 * SHARED, target, None, OPT_VOCAB))

    def shared_chunk(c, carry):
        shared_ready(c)
        z_buf[...] += shared_dot(c, every)
        return carry

    lax.fori_loop(1, last - 1, shared_chunk, 0)
    shared_ready(last - 1)
    shared_ready(last)
    z_buf[...] += shared_dot(last - 1, every) + shared_dot(last, every)

    pltpu.make_async_remote_copy(tg_recv, tg_recv, ts_sem, tr_sem, device_id={"dp": dp_far, "tp": tp}, device_id_type=MESH).wait_recv()
    far_target = jnp.where(lane < half, tg_recv[0, 0:1, :], tg_recv[1, 0:1, :]).astype(jnp.int32)
    both = jnp.concatenate([target, far_target], axis=1)
    n_blocks = SHARED // BLOCK

    def block(i):
        return z_buf[pl.ds(pl.multiple_of(i * BLOCK, BLOCK), BLOCK), :].reshape(BLOCK // 8, 8, 2 * tokens)

    def add(i, m8, s8, t8):
        zz = block(i)
        step = lax.broadcasted_iota(jnp.int32, zz.shape, 0) * 8
        t8 = t8 + jnp.sum(jnp.where(step == (both - (first_row + shared_row + i * BLOCK) - sub)[None], zz, 0.0), axis=0)
        return s8 + jnp.sum(jnp.exp(zz - m8[None]), axis=0), t8

    def step(i, state):
        m8, s8, t8 = state
        m_new = jnp.maximum(m8, jnp.max(block(i + 1), axis=0))
        s8, t8 = add(i, m8, s8, t8)
        return m_new, s8 * jnp.exp(m8 - m_new), t8

    zero = jnp.zeros((8, 2 * tokens), jnp.float32)
    m8, s8, t8 = lax.fori_loop(0, n_blocks - 1, step, (jnp.max(block(0), axis=0), zero, zero))
    m_h, s_h, t_h = fold((m8, *add(n_blocks - 1, m8, s8, t8)))

    m_o = jnp.maximum(m_s, m_h[:, :tokens])
    s_o = s_s * jnp.exp(m_s - m_o) + s_h[:, :tokens] * jnp.exp(m_h[:, :tokens] - m_o)
    t_o = t_s + t_h[:, :tokens]
    own_send[0:1, :] = m_o
    own_send[1:2, :] = s_o
    own_send[2:3, :] = t_o
    far_send[0:1, :] = m_h[:, tokens:]
    far_send[1:2, :] = s_h[:, tokens:]
    far_send[2:3, :] = t_h[:, tokens:]

    copies = []
    for i, (d, k) in enumerate(group):
        slot = k - 1 if i < n_tp - 1 else (n_tp - 1 + k if i < 2 * n_tp - 1 else 2 * n_tp - 1 + k)
        copies.append(pltpu.make_async_remote_copy(own_send if i < n_tp - 1 else far_send, all_recv.at[slot], ss_sem, sr_sem, device_id={"dp": d, "tp": (tp + k) % n_tp}, device_id_type=MESH))
    for c in copies[n_tp - 1:] + copies[:n_tp - 1]:
        c.start()

    def total_of(ref, send_sem, recv_sem):
        return pltpu.make_async_remote_copy(ref, ref, send_sem, recv_sem, device_id={"dp": dp, "tp": tp_other}, device_id_type=MESH)

    total_of(hs_buf, hs_sem, sr_sem).wait_send()
    total_of(hs_buf, rs_sem, sr_sem).wait_send()
    total_of(tg_recv, ts_sem, sr_sem).wait_send()
    total_of(all_recv, ss_sem, sr_sem).wait_recv()

    parts = [(m_o, s_o, t_o)]
    for k in range(n_tp - 1):
        parts.append(tuple(all_recv[k, j:j + 1, :] for j in range(3)))
    for k in range(n_tp - 1, 2 * n_tp - 1):
        parts.append(tuple(jnp.where(lane < half, all_recv[k, j:j + 1, :], all_recv[k + n_tp, j:j + 1, :]) for j in range(3)))
    m = functools.reduce(jnp.maximum, [p[0] for p in parts])
    total = sum(p[1] * jnp.exp(p[0] - m) for p in parts)
    z_t = sum(p[2] for p in parts)
    norm = m + jnp.log(total)
    logp = (z_t - norm) * msk_ref[...].astype(jnp.float32)
    out_ref[0:1, :] = norm
    out_ref[1:2, :] = logp
    out_ref[2:3, :] = m - norm
    total_of(all_recv, ss_sem, sr_sem).wait_send()


def finish(all_ref, norm_ref, logp_ref, seq_ref, top_ref):
    logp = all_ref[1:2, :]
    norm_ref[...] = all_ref[0:1, :]
    logp_ref[...] = logp
    top_ref[...] = all_ref[2:3, :]
    seq_ref[...] = jnp.sum(logp, axis=-1, keepdims=True)


def solution(mesh):
    n_tp = mesh.shape["tp"]

    def local_part(hidden, ln_gain, ln_bias, embedding, targets, score_mask):
        _, tokens, width = hidden.shape
        rows = embedding.shape[0]
        n_slots = width // CHUNK
        single = rows - 2 * SHARED
        vmem = pl.BlockSpec(memory_space=pltpu.VMEM)
        hbm = pl.BlockSpec(memory_space=pl.ANY)
        f32, bf16 = jnp.float32, jnp.bfloat16
        dma = pltpu.SemaphoreType.DMA
        n_group = 3 * n_tp - 1
        out = pl.pallas_call(
            functools.partial(kernel, n_tp),
            out_shape=pltpu.VMEM((8, tokens), f32),
            in_specs=[hbm] * 6,
            out_specs=vmem,
            scratch_shapes=[
                pltpu.VMEM((1, width), f32),
                pltpu.VMEM((1, width), f32),
                pltpu.VMEM((1, tokens), jnp.int32),
                pltpu.VMEM((1, tokens), jnp.int32),
                pltpu.VMEM((n_slots, tokens, CHUNK), bf16),
                pltpu.VMEM((n_slots, 2 * tokens, CHUNK), bf16),
                pltpu.VMEM((n_slots, tokens // 2, CHUNK), f32),
                pltpu.VMEM((n_slots, tokens, CHUNK), f32),
                pltpu.VMEM((HELD, SHARED, CHUNK), bf16),
                pltpu.VMEM((SHARED, 2 * tokens), f32),
                pltpu.VMEM((single, tokens), f32),
                pltpu.VMEM((8, tokens), f32),
                pltpu.VMEM((2, 8, tokens), f32),
                pltpu.VMEM((8, tokens), f32),
                pltpu.VMEM((8, tokens), f32),
                pltpu.VMEM((n_group, 8, tokens), f32),
                dma((4,)), dma((2,)), dma((n_slots,)), dma((n_slots + 1,)), dma, dma((n_slots + 1,)), dma, dma((n_slots + 1,)),
                dma, dma, dma, dma,
            ],
            compiler_params=pltpu.CompilerParams(collective_id=0, has_side_effects=True, vmem_limit_bytes=63 << 20),
        )(hidden, ln_gain.reshape(1, width), ln_bias.reshape(1, width), embedding, targets, score_mask)
        row = jax.ShapeDtypeStruct((1, tokens), f32)
        norm, logp, seq, top = pl.pallas_call(
            finish, out_shape=(row, row, jax.ShapeDtypeStruct((1, 1), f32), row), in_specs=[vmem], out_specs=(vmem,) * 4,
        )(pltpu.with_memory_space_constraint(out, pltpu.VMEM))
        return norm, logp, seq.reshape(1), top

    row_spec = P("dp", None)
    return jax.shard_map(local_part, mesh=mesh, in_specs=(P("dp", None, None), P(), P(), P("tp", None), row_spec, row_spec), out_specs=(row_spec, row_spec, P("dp"), row_spec), check_vma=False)
```

time: 32.9 us -> 30.7 us (0.933)
  Pallas kernels: 32.2 us -> 29.9 us
    pallas_call x1, Pallas kernels: 31.6 us -> 29.3 us  [local_part(): pl.pallas_call(functools.partial(kernel, n_tp), out_shape=pltpu.VMEM((8,...]
where the time goes in v5:
time: 30.7 us; the launch traced here: 30.6 us
  Pallas kernels  29.9 us (97%)
  between operations  0.64 us (2%)
    pallas_call x1, Pallas kernels, local_part(): pl.pallas_call(functools.partial(kernel, n_tp), out_shape=pltpu.VMEM((8,...  29.3 us

profile of v5, /device:TPU:0, one launch (start us, length us, event | category | flops | bytes accessed | tf_op | source)
XLA Modules:
  0.0 30.6 jit_solution(1872699190522803574)
XLA Ops:
  0.6 29.3 %shard_map.93.all_ref = f32[8,128]{1,0:T(8,128)S(1)} custom-call(bf16[1,128,4096]{2,1,0:T(8,128)(2,1)} %x_hbm.1, f32[1,4096]{1,0:T(1,128)} %bitcast.3, f32[1,4096]{1,0:T(1,128)} %bitcast.4, bf16[12672,4096]{1,0:T(8,128)(2,1)} %emb_hbm.1, s32[1,128]{1,0:T(1,128)} %tgt_hbm.1, s32[1,128]{1,0:T(1,128)} %msk_hbm.1), custom_call_target="tpu_custom_call" | custom-call | tf_op jit(solution)/shard_map/pallas_call | solution.py:335
  30.0 0.6 %shard_map.94 = (f32[1,128]{1,0:T(1,128)}, f32[1,128]{1,0:T(1,128)}, f32[1,1]{1,0:T(1,128)}, f32[1,128]{1,0:T(1,128)}) custom-call(f32[8,128]{1,0:T(8,128)S(1)} %shard_map.93.all_ref), custom_call_target="tpu_custom_call" | custom-call | tf_op jit(solution)/shard_map/pallas_call | solution.py:363

commit v6 on v5

--- a/solution.py
+++ b/solution.py
@@ -248,44 +248,43 @@
 
     pltpu.make_async_remote_copy(tg_recv, tg_recv, ts_sem, tr_sem, device_id={"dp": dp_far, "tp": tp}, device_id_type=MESH).wait_recv()
     far_target = jnp.where(lane < half, tg_recv[0, 0:1, :], tg_recv[1, 0:1, :]).astype(jnp.int32)
-    both = jnp.concatenate([target, far_target], axis=1)
     n_blocks = SHARED // BLOCK
 
-    def block(i):
-        return z_buf[pl.ds(pl.multiple_of(i * BLOCK, BLOCK), BLOCK), :].reshape(BLOCK // 8, 8, 2 * tokens)
-
-    def add(i, m8, s8, t8):
-        zz = block(i)
-        step = lax.broadcasted_iota(jnp.int32, zz.shape, 0) * 8
-        t8 = t8 + jnp.sum(jnp.where(step == (both - (first_row + shared_row + i * BLOCK) - sub)[None], zz, 0.0), axis=0)
-        return s8 + jnp.sum(jnp.exp(zz - m8[None]), axis=0), t8
-
-    def step(i, state):
-        m8, s8, t8 = state
-        m_new = jnp.maximum(m8, jnp.max(block(i + 1), axis=0))
-        s8, t8 = add(i, m8, s8, t8)
-        return m_new, s8 * jnp.exp(m8 - m_new), t8
-
-    zero = jnp.zeros((8, 2 * tokens), jnp.float32)
-    m8, s8, t8 = lax.fori_loop(0, n_blocks - 1, step, (jnp.max(block(0), axis=0), zero, zero))
-    m_h, s_h, t_h = fold((m8, *add(n_blocks - 1, m8, s8, t8)))
-
-    m_o = jnp.maximum(m_s, m_h[:, :tokens])
-    s_o = s_s * jnp.exp(m_s - m_o) + s_h[:, :tokens] * jnp.exp(m_h[:, :tokens] - m_o)
-    t_o = t_s + t_h[:, :tokens]
-    own_send[0:1, :] = m_o
-    own_send[1:2, :] = s_o
-    own_send[2:3, :] = t_o
-    far_send[0:1, :] = m_h[:, tokens:]
-    far_send[1:2, :] = s_h[:, tokens:]
-    far_send[2:3, :] = t_h[:, tokens:]
-
-    copies = []
-    for i, (d, k) in enumerate(group):
-        slot = k - 1 if i < n_tp - 1 else (n_tp - 1 + k if i < 2 * n_tp - 1 else 2 * n_tp - 1 + k)
-        copies.append(pltpu.make_async_remote_copy(own_send if i < n_tp - 1 else far_send, all_recv.at[slot], ss_sem, sr_sem, device_id={"dp": d, "tp": (tp + k) % n_tp}, device_id_type=MESH))
-    for c in copies[n_tp - 1:] + copies[:n_tp - 1]:
-        c.start()
+    def shared_stats(first_lane, target):
+        def block(i):
+            return z_buf[pl.ds(pl.multiple_of(i * BLOCK, BLOCK), BLOCK), first_lane:first_lane + tokens].reshape(BLOCK // 8, 8, tokens)
+
+        def add(i, m8, s8, t8):
+            zz = block(i)
+            step = lax.broadcasted_iota(jnp.int32, zz.shape, 0) * 8
+            t8 = t8 + jnp.sum(jnp.where(step == (target - (first_row + shared_row + i * BLOCK) - sub)[None], zz, 0.0), axis=0)
+            return s8 + jnp.sum(jnp.exp(zz - m8[None]), axis=0), t8
+
+        def step(i, state):
+            m8, s8, t8 = state
+            m_new = jnp.maximum(m8, jnp.max(block(i + 1), axis=0))
+            s8, t8 = add(i, m8, s8, t8)
+            return m_new, s8 * jnp.exp(m8 - m_new), t8
+
+        zero = jnp.zeros((8, tokens), jnp.float32)
+        m8, s8, t8 = lax.fori_loop(0, n_blocks - 1, step, (jnp.max(block(0), axis=0), zero, zero))
+        return fold((m8, *add(n_blocks - 1, m8, s8, t8)))
+
+    def send_stats(src, first, end):
+        for i, (d, k) in list(enumerate(group))[first:end]:
+            slot = k - 1 if i < n_tp - 1 else (n_tp - 1 + k if i < 2 * n_tp - 1 else 2 * n_tp - 1 + k)
+            pltpu.make_async_remote_copy(src, all_recv.at[slot], ss_sem, sr_sem, device_id={"dp": d, "tp": (tp + k) % n_tp}, device_id_type=MESH).start()
+
+    for j, v in enumerate(shared_stats(tokens, far_target)):
+        far_send[j:j + 1, :] = v
+    send_stats(far_send, n_tp - 1, len(group))
+    m_h, s_h, t_h = shared_stats(0, target)
+    m_o = jnp.maximum(m_s, m_h)
+    s_o = s_s * jnp.exp(m_s - m_o) + s_h * jnp.exp(m_h - m_o)
+    t_o = t_s + t_h
+    for j, v in enumerate((m_o, s_o, t_o)):
+        own_send[j:j + 1, :] = v
+    send_stats(own_send, 0, n_tp - 1)
 
     def total_of(ref, send_sem, recv_sem):
         return pltpu.make_async_remote_copy(ref, ref, send_sem, recv_sem, device_id={"dp": dp, "tp": tp_other}, device_id_type=MESH)

time: 30.7 us -> 30.1 us (0.980)
  Pallas kernels: 29.9 us -> 29.3 us
    pallas_call x1, Pallas kernels: 29.3 us -> 28.7 us  [local_part(): pl.pallas_call(functools.partial(kernel, n_tp), out_shape=pltpu.VMEM((8,...]
where the time goes in v6:
time: 30.1 us; the launch traced here: 30 us
  Pallas kernels  29.3 us (97%)
  between operations  0.64 us (2%)
    pallas_call x1, Pallas kernels, local_part(): pl.pallas_call(functools.partial(kernel, n_tp), out_shape=pltpu.VMEM((8,...  28.7 us

profile of v6, /device:TPU:0, one launch (start us, length us, event | category | flops | bytes accessed | tf_op | source)
XLA Modules:
  0.0 30.0 jit_solution(4333744968935116550)
XLA Ops:
  0.6 28.7 %shard_map.93.all_ref = f32[8,128]{1,0:T(8,128)S(1)} custom-call(bf16[1,128,4096]{2,1,0:T(8,128)(2,1)} %x_hbm.1, f32[1,4096]{1,0:T(1,128)} %bitcast.3, f32[1,4096]{1,0:T(1,128)} %bitcast.4, bf16[12672,4096]{1,0:T(8,128)(2,1)} %emb_hbm.1, s32[1,128]{1,0:T(1,128)} %tgt_hbm.1, s32[1,128]{1,0:T(1,128)} %msk_hbm.1), custom_call_target="tpu_custom_call" | custom-call | tf_op jit(solution)/shard_map/pallas_call | solution.py:334
  29.4 0.6 %shard_map.94 = (f32[1,128]{1,0:T(1,128)}, f32[1,128]{1,0:T(1,128)}, f32[1,1]{1,0:T(1,128)}, f32[1,128]{1,0:T(1,128)}) custom-call(f32[8,128]{1,0:T(8,128)S(1)} %shard_map.93.all_ref), custom_call_target="tpu_custom_call" | custom-call | tf_op jit(solution)/shard_map/pallas_call | solution.py:362

commit v7 on v6

--- a/solution.py
+++ b/solution.py
@@ -11,9 +11,9 @@
 LN_EPS = 1e-5
 CHUNK = 512
 SHARED = 5632
-BLOCK = 352
+BLOCK = 256
 HELD = 7
-NORM_ROWS = 32
+NORM_ROWS = 64
 MESH = pl.DeviceIdType.MESH
 NEG_INF = float("-inf")
 NT = (((1,), (1,)), ((), ()))
@@ -43,11 +43,12 @@
     mine = pl.ds(pl.multiple_of(core * half, half), half)
     rest = pl.ds(pl.multiple_of((1 - core) * half, half), half)
 
-    def place(c):
-        if isinstance(c, int) and c in (0, last):
-            return 0, pl.ds(0 if c == 0 else short, short), pl.ds(0 if c == 0 else width - short, short)
-        start = c * CHUNK - short
-        return c, pl.ds(0, CHUNK), pl.ds(start if isinstance(c, int) else pl.multiple_of(start, short), CHUNK)
+    def place(c, halves=False):
+        if halves or (isinstance(c, int) and c < 2):
+            lanes = pl.ds(c * short if isinstance(c, int) else pl.multiple_of(c * short, short), short)
+            return 0, lanes, lanes
+        start = (c - 1) * CHUNK
+        return c - 1, pl.ds(0, CHUNK), pl.ds(start if isinstance(c, int) else pl.multiple_of(start, CHUNK), CHUNK)
 
     def fetch_x(c, part, sl):
         slot, lanes, cols = place(c)
@@ -73,16 +74,16 @@
     def held(c):
         return n_slots - n_held if isinstance(c, int) and n_held <= c < last else c
 
-    def fetch_shared(c):
-        slot, lanes, cols = place(c)
+    def fetch_shared(c, halves=False):
+        slot, lanes, cols = place(c, halves)
         return pltpu.make_async_copy(emb_hbm.at[pl.ds(shared_row, SHARED), cols], e_buf.at[held(slot), :, lanes], e_sem.at[c])
 
     def send_h(c):
         slot, lanes, _ = place(c)
         return pltpu.make_async_remote_copy(hs_buf.at[slot, :, lanes], fr_buf.at[slot, mine, lanes], hs_sem, hr_sem.at[c], device_id={"dp": dp_far, "tp": tp}, device_id_type=MESH)
 
-    def relay_h(c):
-        slot, lanes, _ = place(c)
+    def relay_h(c, halves=False):
+        slot, lanes, _ = place(c, halves)
         ref = fr_buf.at[slot, mine, lanes]
         return pltpu.make_async_remote_copy(ref, ref, rs_sem, rr_sem.at[c], device_id={"dp": dp, "tp": tp_other}, device_id_type=MESH)
 
@@ -97,7 +98,7 @@
             fetch_x(c, part, sl).start()
     for c in small:
         c.start()
-    for c in (0, last, 1, 2, 3):
+    for c in range(5):
         fetch_single(c).start(priority=1)
 
     barrier = pltpu.get_barrier_semaphore()
@@ -109,9 +110,9 @@
     tg_send[...] = jnp.broadcast_to(tgt_ref[...].astype(jnp.float32), tg_send.shape)
 
     wait_x(0, mine)
-    for c in range(4, last):
+    for c in range(5, last + 1):
         fetch_single(c).start(priority=1)
-    for c in range(2):
+    for c in range(3):
         fetch_shared(c).start(priority=1)
 
     def norm_rows(row):
@@ -121,9 +122,7 @@
             return x_buf[k, sl, :].astype(jnp.float32)
 
         def cols(ref, k):
-            if k == 0:
-                return jnp.concatenate([ref[:, 0:short], ref[:, width - short:width]], axis=1)
-            return ref[:, k * CHUNK - short:(k + 1) * CHUNK - short]
+            return ref[:, k * CHUNK:(k + 1) * CHUNK]
 
         mean = jnp.sum(sum(load(k) for k in range(n_slots)), axis=-1, keepdims=True) / width
         var = jnp.sum(sum((load(k) - mean) * (load(k) - mean) for k in range(n_slots)), axis=-1, keepdims=True) / width
@@ -161,7 +160,7 @@
     def single_step(i, carry):
         @pl.when(i == 2)
         def _():
-            fetch_shared(2).start(priority=1)
+            fetch_shared(3).start(priority=1)
 
         @pl.when(i == 3)
         def _():
@@ -195,39 +194,37 @@
         m1 = jnp.max(state[0], axis=0, keepdims=True)
         return m1, jnp.sum(state[1] * jnp.exp(state[0] - m1), axis=0, keepdims=True), jnp.sum(state[2], axis=0, keepdims=True)
 
-    def shared_ready(c):
-        fetch_shared(c).wait()
+    def pass_on(c):
+        send_h(c).wait_recv()
+        relay_h(c).start()
+
+    def shared_ready(c, halves=False):
+        fetch_shared(c, halves).wait()
         if isinstance(c, int):
-            if c + 2 <= last:
-                send_h(c + 1).wait_recv()
-                relay_h(c + 1).start()
-            if c + 3 <= last:
-                fetch_shared(c + 3).start(priority=1)
+            if c + 1 <= last:
+                pass_on(c + 1)
+            if c + 4 <= last:
+                fetch_shared(c + 4).start(priority=1)
+        elif halves:
+            pass_on(2)
+            fetch_shared(5).start(priority=1)
         else:
-            @pl.when(c + 1 < last)
+            pass_on(c + 1)
+
+            @pl.when(c + 4 < n_held)
             def _():
-                send_h(c + 1).wait_recv()
-                relay_h(c + 1).start()
-
-            @pl.when(c + 2 == last)
-            def _():
-                send_h(last).wait_recv()
-                relay_h(last).start()
-
-            @pl.when(c + 3 < n_held)
-            def _():
-                fetch_shared(c + 3).start(priority=1)
+                fetch_shared(c + 4).start(priority=1)
 
             for k in range(n_held, last + 1):
-                @pl.when(c + 3 == k)
+                @pl.when(c + 4 == k)
                 def _():
                     fetch_shared(k).start(priority=1)
-        relay_h(c).wait_recv()
-        slot, lanes, _ = place(c)
+        relay_h(c, halves).wait_recv()
+        slot, lanes, _ = place(c, halves)
         h_buf[slot, tokens:2 * tokens, lanes] = fr_buf[slot, :, lanes].astype(jnp.bfloat16)
 
-    def shared_dot(c, sl):
-        slot, lanes, _ = place(c)
+    def shared_dot(c, sl, halves=False):
+        slot, lanes, _ = place(c, halves)
         return lax.dot_general(e_buf[held(slot), sl, lanes], h_buf[slot, :, lanes], NT, preferred_element_type=jnp.float32)
 
     target = tgt_ref[...]
@@ -241,10 +238,15 @@
         z_buf[...] += shared_dot(c, every)
         return carry
 
-    lax.fori_loop(1, last - 1, shared_chunk, 0)
-    shared_ready(last - 1)
+    def second_half(c, carry):
+        shared_ready(c, True)
+        z_buf[...] += shared_dot(c, every, True)
+        return carry
+
+    lax.fori_loop(1, 2 + dp // 1024, second_half, 0)
+    lax.fori_loop(2, last, shared_chunk, 0)
     shared_ready(last)
-    z_buf[...] += shared_dot(last - 1, every) + shared_dot(last, every)
+    z_buf[...] += shared_dot(last, every)
 
     pltpu.make_async_remote_copy(tg_recv, tg_recv, ts_sem, tr_sem, device_id={"dp": dp_far, "tp": tp}, device_id_type=MESH).wait_recv()
     far_target = jnp.where(lane < half, tg_recv[0, 0:1, :], tg_recv[1, 0:1, :]).astype(jnp.int32)

time: 30.1 us -> 29.8 us (0.990)
  no operation moved by 1% of the time
where the time goes in v7:
time: 29.8 us; the launch traced here: 29.7 us
  Pallas kernels  29.1 us (98%)
  between operations  0.64 us (2%)
    pallas_call x1, Pallas kernels, local_part(): pl.pallas_call(functools.partial(kernel, n_tp), out_shape=pltpu.VMEM((8,...  28.5 us

profile of v7, /device:TPU:0, one launch (start us, length us, event | category | flops | bytes accessed | tf_op | source)
XLA Modules:
  0.0 29.7 jit_solution(10234325576192546383)
XLA Ops:
  0.6 28.5 %shard_map.93.all_ref = f32[8,128]{1,0:T(8,128)S(1)} custom-call(bf16[1,128,4096]{2,1,0:T(8,128)(2,1)} %x_hbm.1, f32[1,4096]{1,0:T(1,128)} %bitcast.3, f32[1,4096]{1,0:T(1,128)} %bitcast.4, bf16[12672,4096]{1,0:T(8,128)(2,1)} %emb_hbm.1, s32[1,128]{1,0:T(1,128)} %tgt_hbm.1, s32[1,128]{1,0:T(1,128)} %msk_hbm.1), custom_call_target="tpu_custom_call" | custom-call | tf_op jit(solution)/shard_map/pallas_call | solution.py:336
  29.1 0.6 %shard_map.94 = (f32[1,128]{1,0:T(1,128)}, f32[1,128]{1,0:T(1,128)}, f32[1,1]{1,0:T(1,128)}, f32[1,128]{1,0:T(1,128)}) custom-call(f32[8,128]{1,0:T(8,128)S(1)} %shard_map.93.all_ref), custom_call_target="tpu_custom_call" | custom-call | tf_op jit(solution)/shard_map/pallas_call | solution.py:364

commit v8 on v7

--- a/solution.py
+++ b/solution.py
@@ -93,13 +93,14 @@
 
     small = [pltpu.make_async_copy(src, dst, in_sem.at[i]) for i, (src, dst) in enumerate(
         [(tgt_hbm, tgt_ref), (gain_hbm, gain_ref), (bias_hbm, bias_ref), (msk_hbm, msk_ref)])]
-    for part, sl in enumerate((mine, rest)):
-        for c in range(last + 1):
-            fetch_x(c, part, sl).start()
+    for c in range(last + 1):
+        fetch_x(c, 0, mine).start()
+    for c in range(5):
+        fetch_single(c).start(priority=1)
     for c in small:
         c.start()
-    for c in range(5):
-        fetch_single(c).start(priority=1)
+    for c in range(last + 1):
+        fetch_x(c, 1, rest).start()
 
     barrier = pltpu.get_barrier_semaphore()
     group = [(dp, k) for k in range(1, n_tp)] + [(dp_y, k) for k in range(n_tp)] + [(dp_z, k) for k in range(n_tp)]

time: 29.8 us -> 29.8 us (level)
  no operation moved by 1% of the time
where the time goes in v8:
time: 29.8 us; the launch traced here: 29.7 us
  Pallas kernels  29.1 us (98%)
  between operations  0.64 us (2%)
    pallas_call x1, Pallas kernels, local_part(): pl.pallas_call(functools.partial(kernel, n_tp), out_shape=pltpu.VMEM((8,...  28.5 us

profile of v8, /device:TPU:0, one launch (start us, length us, event | category | flops | bytes accessed | tf_op | source)
XLA Modules:
  0.0 29.7 jit_solution(2034726102770769175)
XLA Ops:
  0.6 28.5 %shard_map.93.all_ref = f32[8,128]{1,0:T(8,128)S(1)} custom-call(bf16[1,128,4096]{2,1,0:T(8,128)(2,1)} %x_hbm.1, f32[1,4096]{1,0:T(1,128)} %bitcast.3, f32[1,4096]{1,0:T(1,128)} %bitcast.4, bf16[12672,4096]{1,0:T(8,128)(2,1)} %emb_hbm.1, s32[1,128]{1,0:T(1,128)} %tgt_hbm.1, s32[1,128]{1,0:T(1,128)} %msk_hbm.1), custom_call_target="tpu_custom_call" | custom-call | tf_op jit(solution)/shard_map/pallas_call | solution.py:337
  29.1 0.6 %shard_map.94 = (f32[1,128]{1,0:T(1,128)}, f32[1,128]{1,0:T(1,128)}, f32[1,1]{1,0:T(1,128)}, f32[1,128]{1,0:T(1,128)}) custom-call(f32[8,128]{1,0:T(8,128)S(1)} %shard_map.93.all_ref), custom_call_target="tpu_custom_call" | custom-call | tf_op jit(solution)/shard_map/pallas_call | solution.py:365
